TPU v7x, 32 devices: a whole 2x2x4 slice. The times are simulated.
32 devices in a mesh: dp: 16 (over z, x, core), tensor: 2 (over y).
Axes of the slice: x: 2, y: 2, z: 4, core: 2. Of those that a mesh axis runs over, the one named last changes fastest.
Arguments:
- stream: bfloat16 [4, 16384, 768], P(None, ('dp', 'tensor')), may hold values from -6 to 6
- bounds: int32 [4, 16, 2], P(None, 'dp'), may hold values from 256 to 1024, as said below
- prescale: bfloat16 [768], P(('dp', 'tensor')), may hold values from 0.099609375 to 1.8984375
- expansion: bfloat16 [768, 2, 1536], P('dp', None, 'tensor'), may hold values from -0.21875 to 0.21875
- timestep: bfloat16 [768, 24], P('dp', 'tensor'), may hold values from -0.21875 to 0.21875
- selection: bfloat16 [768, 256], P(('dp', 'tensor')), may hold values from -0.21875 to 0.21875
- kernels: bfloat16 [24, 256], P('tensor', 'dp'), may hold values from -3 to 3
- biases: bfloat16 [24, 64], P('tensor', 'dp'), may hold values from -0.5 to 0.5
- stencil: bfloat16 [256, 4], P(('dp', 'tensor')), may hold values from -3 to 3
- baseline: bfloat16 [256], P(('dp', 'tensor')), may hold values from -0.5 to 0.5
- offset: bfloat16 [24], P('tensor'), may hold values from -6.875 to -2.296875
- decays: bfloat16 [24], P('tensor'), may hold values from 0 to 2.765625
- passthrough: bfloat16 [24], P('tensor'), may hold values from 0.5 to 1.5
- rescale: bfloat16 [24, 64], P('tensor', 'dp'), may hold values from 0.099609375 to 1.8984375
- readout: bfloat16 [1536, 768], P('tensor', 'dp'), may hold values from -0.15625 to 0.15625
- cotangent: bfloat16 [4, 16384, 768], P(None, ('dp', 'tensor')), may hold values from -6 to 6
Outputs:
- result: bfloat16 [4, 16384, 768], P(None, ('dp', 'tensor'))
- stream_gradient: bfloat16 [4, 16384, 768], P(None, ('dp', 'tensor'))
- prescale_gradient: float32 [768], P(('dp', 'tensor'))
- expansion_gradient: float32 [768, 2, 1536], P('dp', None, 'tensor')
- timestep_gradient: float32 [768, 24], P('dp', 'tensor')
- selection_gradient: float32 [768, 256], P(('dp', 'tensor'))
- kernels_gradient: float32 [24, 256], P('tensor', 'dp')
- biases_gradient: float32 [24, 64], P('tensor', 'dp')
- stencil_gradient: float32 [256, 4], P(('dp', 'tensor'))
- baseline_gradient: float32 [256], P(('dp', 'tensor'))
- offset_gradient: float32 [24], P('tensor')
- decays_gradient: float32 [24], P('tensor')
- passthrough_gradient: float32 [24], P('tensor')
- rescale_gradient: float32 [24, 64], P('tensor', 'dp')
- readout_gradient: float32 [1536, 768], P('tensor', 'dp')
Inputs may be any that keep to these rules, and one draw needn't show every extreme that they name: bounds[m, s, 0] ends the slot's first sequence, which starts at position 0; positions from there up to bounds[m, s, 1] form a second sequence of 0 or at least 256 positions; positions after bounds[m, s, 1] are padding. In each micro-batch one slot is filled by one sequence of 1024 positions and another holds a single sequence of 256.
All inputs are finite; a program needn't handle non-finite values.
Results may differ from a plain program's by a relative error of at most 0.022.
Values may be sent and summed in bfloat16 or wider, within the bound.
A program may use at most 512 MiB of HBM per device.

v0:
```python
import jax
import jax.numpy as jnp
from jax import lax
from jax.sharding import PartitionSpec as P

WIDTH = 768
HEAD_DIM = 64
STATE = 128
TAPS = 4
STRETCH = 256
INNER = 1536
SLOT = 1024


epsilon = 1e-05
highest = lax.Precision.HIGHEST


def row_norm(rows, gain):
    return rows * lax.rsqrt(jnp.mean(rows * rows, axis=-1, keepdims=True) + epsilon) * gain


def segments(limits):
    position = jnp.arange(SLOT, dtype=jnp.int32)[None, :]
    first = limits[:, 0:1]
    used = limits[:, 1:2]
    segment = (position >= first).astype(jnp.int32) + (position >= used).astype(jnp.int32)
    live = (position < used).astype(jnp.float32)
    return (segment, live)


def mix_taps(signal, taps, shifts, segment):
    width = taps.shape[1]
    length = signal.shape[1]
    total = shifts + signal * taps[:, width - 1]
    for back in range(1, width):
        moved = jnp.pad(signal, ((0, 0), (back, 0), (0, 0)))[:, :length]
        earlier = jnp.pad(segment, ((0, 0), (back, 0)), constant_values=-1)[:, :length]
        same = (earlier == segment)[:, :, None]
        total = total + jnp.where(same, moved, 0.0) * taps[:, width - 1 - back]
    return jax.nn.silu(total)


def decay_table(cumulative, segment):
    length = cumulative.shape[1]
    order = jnp.arange(length)
    mask = (order[:, None] >= order[None, :])[None] & (segment[:, :, None] == segment[:, None, :])
    mask = mask[:, None]
    spread = jnp.transpose(cumulative, (0, 2, 1))
    gap = spread[:, :, :, None] - spread[:, :, None, :]
    return jnp.where(mask, jnp.exp(jnp.where(mask, gap, 0.0)), 0.0)


def carry_part(reader, entry, scaled, cumulative, segment):
    count = cumulative.shape[0]
    last = segment[:, -1:]
    weight = jnp.where(
        (segment == last)[:, :, None], jnp.exp(cumulative[:, -1:, :] - cumulative), 0.0
    )
    states = jnp.einsum("cjn,cjhp->chnp", entry, scaled * weight[:, :, :, None], precision=highest)
    carry = states[0]
    pieces = [jnp.zeros_like(scaled[0])]
    for index in range(1, count):
        inside = (segment[index] == segment[index - 1, -1]).astype(cumulative.dtype)
        factor = jnp.exp(cumulative[index]) * inside[:, None]
        pieces.append(
            jnp.einsum("in,hnp->ihp", reader[index], carry, precision=highest) * factor[:, :, None]
        )
        carry = carry * (jnp.exp(cumulative[index, -1]) * inside[-1])[:, None, None] + states[index]
    return jnp.stack(pieces)


def step_rates(step_raw, offset, decays):
    step = jax.nn.softplus(step_raw + offset)
    return (step, -jnp.exp(decays) * step)


def slot_forward(scaled, entry, reader, cumulative, segment):
    table = decay_table(cumulative, segment)
    inner = jnp.einsum("cin,cjn->cij", reader, entry, preferred_element_type=jnp.float32)
    weights = (inner[:, None] * table).astype(jnp.bfloat16)
    diagonal = jnp.einsum("chij,cjhp->cihp", weights, scaled, preferred_element_type=jnp.float32)
    carried = carry_part(
        reader.astype(jnp.float32),
        entry.astype(jnp.float32),
        scaled.astype(jnp.float32),
        cumulative,
        segment,
    )
    return diagonal + carried


def slot_backward(scaled, entry, reader, cumulative, segment, back):
    table, table_pull = jax.vjp(lambda values: decay_table(values, segment), cumulative)
    inner = jnp.einsum("cin,cjn->cij", reader, entry, preferred_element_type=jnp.float32)
    weights = (inner[:, None] * table).astype(jnp.bfloat16)
    back_weights = jnp.einsum("cihp,cjhp->chij", back, scaled, preferred_element_type=jnp.float32)
    back_scaled = jnp.einsum("chij,cihp->cjhp", weights, back, preferred_element_type=jnp.float32)
    back_inner = jnp.sum(back_weights * table, axis=1).astype(jnp.bfloat16)
    back_reader = jnp.einsum("cij,cjn->cin", back_inner, entry, preferred_element_type=jnp.float32)
    back_entry = jnp.einsum("cij,cin->cjn", back_inner, reader, preferred_element_type=jnp.float32)
    (back_cumulative,) = table_pull(back_weights * inner[:, None])
    carried, carry_pull = jax.vjp(
        lambda first, second, third, fourth: carry_part(first, second, third, fourth, segment),
        reader.astype(jnp.float32),
        entry.astype(jnp.float32),
        scaled.astype(jnp.float32),
        cumulative,
    )
    more_reader, more_entry, more_scaled, more_cumulative = carry_pull(back.astype(jnp.float32))
    return (
        back_scaled + more_scaled,
        back_entry + more_entry,
        back_reader + more_reader,
        back_cumulative + more_cumulative,
    )


def reduce_gradients(head_terms, shared_terms, scalar_terms):
    heads_done = (
        lax.psum_scatter(
            head_terms[0].astype(jnp.bfloat16), "dp", scatter_dimension=0, tiled=True
        ).astype(jnp.float32),
        lax.psum_scatter(
            head_terms[1].astype(jnp.bfloat16), "dp", scatter_dimension=0, tiled=True
        ).astype(jnp.float32),
        lax.psum_scatter(
            head_terms[2].astype(jnp.bfloat16), "dp", scatter_dimension=1, tiled=True
        ).astype(jnp.float32),
        lax.psum_scatter(
            head_terms[3].astype(jnp.bfloat16), "dp", scatter_dimension=1, tiled=True
        ).astype(jnp.float32),
        lax.psum_scatter(
            head_terms[4].astype(jnp.bfloat16), "dp", scatter_dimension=1, tiled=True
        ).astype(jnp.float32),
        lax.psum_scatter(
            head_terms[5].astype(jnp.bfloat16), "dp", scatter_dimension=1, tiled=True
        ).astype(jnp.float32),
    )
    shared_done = (
        lax.psum_scatter(shared_terms[0], ("dp", "tensor"), scatter_dimension=0, tiled=True),
        lax.psum_scatter(shared_terms[1], ("dp", "tensor"), scatter_dimension=0, tiled=True),
        lax.psum_scatter(shared_terms[2], ("dp", "tensor"), scatter_dimension=0, tiled=True),
        lax.psum_scatter(shared_terms[3], ("dp", "tensor"), scatter_dimension=0, tiled=True),
    )
    scalars_done = lax.psum(scalar_terms, "dp")
    return (heads_done, shared_done, scalars_done)


def local(
    stream,
    bounds,
    prescale,
    expansion,
    timestep,
    selection,
    kernels,
    biases,
    stencil,
    baseline,
    offset,
    decays,
    passthrough,
    rescale,
    readout,
    cotangent,
):
    expand_full, time_full, kernel_full, bias_full, rescale_full, readout_full = (
        lax.all_gather(expansion, "dp", axis=0, tiled=True),
        lax.all_gather(timestep, "dp", axis=0, tiled=True),
        lax.all_gather(kernels, "dp", axis=1, tiled=True),
        lax.all_gather(biases, "dp", axis=1, tiled=True),
        lax.all_gather(rescale, "dp", axis=1, tiled=True),
        lax.all_gather(readout, "dp", axis=1, tiled=True),
    )
    select_full, stencil_full, baseline_full, prescale_full = (
        lax.all_gather(selection, ("dp", "tensor"), axis=0, tiled=True),
        lax.all_gather(stencil, ("dp", "tensor"), axis=0, tiled=True),
        lax.all_gather(baseline, ("dp", "tensor"), axis=0, tiled=True),
        lax.all_gather(prescale, ("dp", "tensor"), axis=0, tiled=True),
    )
    local_heads = offset.shape[0]
    local_inner = local_heads * HEAD_DIM
    joined = jnp.concatenate([expand_full.reshape(WIDTH, 2 * local_inner), time_full], axis=1)
    taps = jnp.concatenate([kernel_full.reshape(local_inner, TAPS), stencil_full], axis=0).astype(
        jnp.float32
    )
    shifts = jnp.concatenate([bias_full.reshape(local_inner), baseline_full]).astype(jnp.float32)
    prescale_f = prescale_full.astype(jnp.float32)
    rescale_f = rescale_full.reshape(local_inner).astype(jnp.float32)
    offset_f = offset.astype(jnp.float32)
    decays_f = decays.astype(jnp.float32)
    passthrough_f = passthrough.astype(jnp.float32)
    rows = stream.shape[1]
    place = lax.axis_index("tensor")
    span = rows * lax.axis_size("tensor")
    slot_count = span // SLOT
    stretches = SLOT // STRETCH
    order = jnp.arange(STRETCH)
    lower_ones = (order[:, None] >= order[None, :]).astype(jnp.float32)
    block_shape = (slot_count, stretches, STRETCH)
    results = []
    gradients = []
    totals = None
    for micro in range(stream.shape[0]):
        rows_in = stream[micro].astype(jnp.float32)
        segment, live = segments(bounds[micro])
        live_own = lax.dynamic_slice_in_dim(live.reshape(span), place * rows, rows)
        normed_own, norm_pull = jax.vjp(row_norm, rows_in, prescale_f)
        lowered = normed_own.astype(jnp.bfloat16)
        lowered_all = lax.all_gather(lowered, "tensor", axis=0, tiled=True)
        chosen_all = jnp.dot(lowered_all, select_full, preferred_element_type=jnp.float32).astype(
            jnp.bfloat16
        )
        projected = jnp.dot(lowered_all, joined, preferred_element_type=jnp.float32)
        gate = projected[:, :local_inner]
        inner_in = projected[:, local_inner : 2 * local_inner]
        step_raw = projected[:, 2 * local_inner :]
        signal = jnp.concatenate([inner_in, chosen_all.astype(jnp.float32)], axis=1)
        signal = signal.reshape(slot_count, SLOT, local_inner + 2 * STATE)
        mixed, mix_pull = jax.vjp(
            lambda values, weights, shift: mix_taps(values, weights, shift, segment),
            signal,
            taps,
            shifts,
        )
        mixed = mixed.reshape(span, local_inner + 2 * STATE)
        convolved = mixed[:, :local_inner].reshape(span, local_heads, HEAD_DIM)
        entry = mixed[:, local_inner : local_inner + STATE].astype(jnp.bfloat16)
        reader = mixed[:, local_inner + STATE :].astype(jnp.bfloat16)
        (step, rate), rate_pull = jax.vjp(step_rates, step_raw, offset_f, decays_f)
        scaled = (convolved * step[:, :, None]).astype(jnp.bfloat16)
        cumulative = jnp.einsum(
            "ij,scjh->scih",
            lower_ones,
            rate.reshape(block_shape + (local_heads,)),
            precision=highest,
        )
        blocks = (
            scaled.reshape(block_shape + (local_heads, HEAD_DIM)),
            entry.reshape(block_shape + (STATE,)),
            reader.reshape(block_shape + (STATE,)),
            cumulative,
            segment.reshape(block_shape),
        )
        core = lax.map(lambda items: slot_forward(*items), blocks)
        output = core.reshape(span, local_heads, HEAD_DIM) + passthrough_f[:, None] * convolved
        output = output.reshape(span, local_inner)
        gated, gate_pull = jax.vjp(lambda values, gates: values * jax.nn.silu(gates), output, gate)
        squares = lax.psum(jnp.sum(gated * gated, axis=1), "tensor")
        inverse = lax.rsqrt(squares / INNER + epsilon)[:, None]
        lifted_low = (gated * inverse * rescale_f).astype(jnp.bfloat16)
        mixer = lax.psum_scatter(
            jnp.dot(lifted_low, readout_full, preferred_element_type=jnp.float32).astype(
                jnp.bfloat16
            ),
            "tensor",
            scatter_dimension=0,
            tiled=True,
        ).astype(jnp.float32)
        results.append((rows_in + live_own[:, None] * mixer).astype(jnp.bfloat16))
        back_rows = jnp.where(
            live_own[:, None] > 0, cotangent[micro], jnp.zeros_like(cotangent[micro])
        )
        back_all = lax.all_gather(back_rows, "tensor", axis=0, tiled=True)
        readout_term = jnp.einsum(
            "sc,sd->cd", lifted_low, back_all, preferred_element_type=jnp.float32
        )
        back_lifted = jnp.einsum(
            "sd,cd->sc", back_all, readout_full, preferred_element_type=jnp.float32
        )
        rescale_term = jnp.sum(back_lifted * gated * inverse, axis=0)
        weighted = back_lifted * rescale_f
        dots = lax.psum(jnp.sum(weighted * gated, axis=1), "tensor")
        back_gated = (
            inverse * weighted - gated * (inverse * inverse * inverse) * (dots / INNER)[:, None]
        )
        back_output, back_gate = gate_pull(back_gated)
        back_output = back_output.astype(jnp.bfloat16)
        back_heads = back_output.astype(jnp.float32).reshape(span, local_heads, HEAD_DIM)
        passthrough_term = jnp.sum(back_heads * convolved, axis=(0, 2))
        back_blocks = blocks + (back_output.reshape(block_shape + (local_heads, HEAD_DIM)),)
        back_scaled, back_entry, back_reader, back_cumulative = lax.map(
            lambda items: slot_backward(*items), back_blocks
        )
        back_scaled = back_scaled.reshape(span, local_heads, HEAD_DIM)
        back_rate = jnp.einsum("ij,scih->scjh", lower_ones, back_cumulative, precision=highest)
        back_rate = back_rate.reshape(span, local_heads)
        back_step = jnp.sum(back_scaled * convolved, axis=2)
        back_convolved = passthrough_f[:, None] * back_heads + back_scaled * step[:, :, None]
        back_raw, offset_term, decays_term = rate_pull((back_step, back_rate))
        back_mixed = jnp.concatenate(
            [
                back_convolved.reshape(span, local_inner),
                back_entry.reshape(span, STATE),
                back_reader.reshape(span, STATE),
            ],
            axis=1,
        )
        back_signal, back_taps, back_shifts = mix_pull(
            back_mixed.reshape(slot_count, SLOT, local_inner + 2 * STATE)
        )
        back_signal = back_signal.reshape(span, local_inner + 2 * STATE)
        back_projected = jnp.concatenate(
            [back_gate, back_signal[:, :local_inner], back_raw], axis=1
        )
        back_projected = back_projected.astype(jnp.bfloat16)
        joined_term = jnp.einsum(
            "sd,sk->dk", lowered_all, back_projected, preferred_element_type=jnp.float32
        )
        back_lowered = jnp.einsum(
            "sk,dk->sd", back_projected, joined, preferred_element_type=jnp.float32
        )
        own_lowered, own_chosen = (
            lax.psum_scatter(
                back_lowered.astype(jnp.bfloat16), "tensor", scatter_dimension=0, tiled=True
            ).astype(jnp.float32),
            lax.psum_scatter(
                back_signal[:, local_inner:].astype(jnp.bfloat16),
                "tensor",
                scatter_dimension=0,
                tiled=True,
            ).astype(jnp.float32),
        )
        chosen_low = own_chosen.astype(jnp.bfloat16)
        select_term = jnp.einsum(
            "sd,sk->dk", lowered, chosen_low, preferred_element_type=jnp.float32
        )
        own_lowered = own_lowered + jnp.einsum(
            "sk,dk->sd", chosen_low, select_full, preferred_element_type=jnp.float32
        )
        back_stream, prescale_term = norm_pull(own_lowered)
        gradients.append((cotangent[micro].astype(jnp.float32) + back_stream).astype(jnp.bfloat16))
        head_terms = (
            joined_term[:, : 2 * local_inner].reshape(WIDTH, 2, local_inner),
            joined_term[:, 2 * local_inner :],
            back_taps[:local_inner].reshape(local_heads, HEAD_DIM * TAPS),
            back_shifts[:local_inner].reshape(local_heads, HEAD_DIM),
            rescale_term.reshape(local_heads, HEAD_DIM),
            readout_term,
        )
        shared_terms = (
            select_term,
            back_taps[local_inner:],
            back_shifts[local_inner:],
            prescale_term,
        )
        scalar_terms = (offset_term, decays_term, passthrough_term)
        terms = (head_terms, shared_terms, scalar_terms)
        totals = terms if totals is None else jax.tree.map(jnp.add, totals, terms)
    totals = reduce_gradients(totals[0], totals[1], totals[2])
    heads_done, shared_done, scalars_done = totals
    return (
        jnp.stack(results),
        jnp.stack(gradients),
        shared_done[3],
        heads_done[0],
        heads_done[1],
        shared_done[0],
        heads_done[2],
        heads_done[3],
        shared_done[1],
        shared_done[2],
        scalars_done[0],
        scalars_done[1],
        scalars_done[2],
        heads_done[4],
        heads_done[5],
    )


def solution(mesh):
    placed = (
        P(None, ("dp", "tensor"), None),
        P(None, "dp", None),
        P(("dp", "tensor")),
        P("dp", None, "tensor"),
        P("dp", "tensor"),
        P(("dp", "tensor"), None),
        P("tensor", "dp"),
        P("tensor", "dp"),
        P(("dp", "tensor"), None),
        P(("dp", "tensor")),
        P("tensor"),
        P("tensor"),
        P("tensor"),
        P("tensor", "dp"),
        P("tensor", "dp"),
        P(None, ("dp", "tensor"), None),
    )
    return jax.shard_map(
        local,
        mesh=mesh,
        in_specs=placed,
        out_specs=(
            P(None, ("dp", "tensor"), None),
            P(None, ("dp", "tensor"), None),
            P(("dp", "tensor")),
            P("dp", None, "tensor"),
            P("dp", "tensor"),
            P(("dp", "tensor"), None),
            P("tensor", "dp"),
            P("tensor", "dp"),
            P(("dp", "tensor"), None),
            P(("dp", "tensor")),
            P("tensor"),
            P("tensor"),
            P("tensor"),
            P("tensor", "dp"),
            P("tensor", "dp"),
        ),
        check_vma=False,
    )
```

profile of v0, /device:TPU:0, one launch (start us, length us, event | category | flops | bytes accessed | tf_op | source)
XLA Modules:
  0.0 1634.4 jit_solution(13153329895974586795)
XLA Ops:
  9.1 42.0 %all-reduce.112 = (bf16[768]{0:T(1024)(128)(2,1)S(1)}, bf16[256]{0:T(256)(128)(2,1)S(1)}) all-reduce(bf16[768]{0:T(1024)(128)(2,1)S(1)} %dynamic-update-slice.1, bf16[256]{0:T(256)(128)(2,1)S(1)} %dynamic-update-slice), channel_id=1, replica_groups=mesh['dp'=16,'tensor'=2] {'dp','tensor'}, use_global_device_ids=true, to_apply=%add.101 | all-reduce | flops 1024 | bytes 4096
  83.2 21.1 %all-gather.1 = bf16[16,48,12]{1,2,0:T(8,128)(2,1)S(1)} all-gather(bf16[1,48,12]{1,2,0:T(8,128)(2,1)S(1)} %bitcast.1491), channel_id=1, replica_groups=mesh['dp'=16,'tensor'=2] {'dp'}, dimensions={0}, use_global_device_ids=true | all-gather | bytes 19584 | tf_op jit(solution)/shard_map/all_gather | solution.py:170
  104.6 67.0 %all_gather.60 = bf16[768,256]{1,0:T(8,128)(2,1)S(1)} all-gather(bf16[24,256]{1,0:T(8,128)(2,1)S(1)} %copy-done.424), channel_id=1, replica_groups=mesh['dp'=16,'tensor'=2] {'dp','tensor'}, dimensions={0}, use_global_device_ids=true | all-gather | bytes 405504 | tf_op jit(solution)/shard_map/all_gather | solution.py:177
  171.8 17.2 %all-gather = bf16[16,4,12]{2,1,0:T(4,128)(2,1)S(1)} all-gather(bf16[1,4,12]{2,1,0:T(4,128)(2,1)S(1)} %bitcast.1494), channel_id=1, replica_groups=mesh['dp'=16,'tensor'=2] {'dp'}, dimensions={0}, use_global_device_ids=true | all-gather | bytes 1632 | tf_op jit(solution)/shard_map/all_gather | solution.py:172
  189.2 19.2 %all_gather.61 = bf16[12,256]{0,1:T(8,128)(2,1)S(1)} all-gather(bf16[12,16]{0,1:T(8,128)(2,1)S(1)} %copy.701), channel_id=1, replica_groups=mesh['dp'=16,'tensor'=2] {'dp'}, dimensions={1}, use_global_device_ids=true | all-gather | bytes 6528 | tf_op jit(solution)/shard_map/all_gather | solution.py:171
  209.1 65.5 %all-gather.2 = bf16[32,8,4]{1,2,0:T(4,128)(2,1)S(1)} all-gather(bf16[1,8,4]{1,2,0:T(4,128)(2,1)S(1)} %bitcast.1495), channel_id=1, replica_groups=mesh['dp'=16,'tensor'=2] {'dp','tensor'}, dimensions={0}, use_global_device_ids=true | all-gather | bytes 2112 | tf_op jit(solution)/shard_map/all_gather | solution.py:178
  302.2 17.4 %all-gather.3 = bf16[16,4,12]{2,1,0:T(4,128)(2,1)S(1)} all-gather(bf16[1,4,12]{2,1,0:T(4,128)(2,1)S(1)} %bitcast.1496), channel_id=1, replica_groups=mesh['dp'=16,'tensor'=2] {'dp'}, dimensions={0}, use_global_device_ids=true | all-gather | bytes 1632 | tf_op jit(solution)/shard_map/all_gather | solution.py:173
  356.2 6.8 fusion.611
  431.1 6.8 fusion.608
  473.3 6.8 fusion.605
  515.1 6.8 fusion.602
  558.0 14.6 multiply_reduce_fusion.35
  572.6 8.6 all-reduce.111
  586.4 11.0 multiply_reduce_fusion.21
  597.4 9.1 all-reduce.110
  607.2 8.6 fusion.88
  622.4 9.5 fusion.7
  648.8 9.4 fusion.5
  675.3 9.9 fusion.9
  697.8 10.8 fusion.11
  804.3 7.7 multiply_reduce_fusion.30
  816.6 8.5 multiply_reduce_fusion.26
  838.6 8.2 multiply_reduce_fusion.24
  889.5 10.8 fusion.89
  903.0 10.4 fusion.586
  913.5 10.5 fusion.585
  924.1 9.9 fusion.588
  934.3 8.5 fusion.587
  944.5 24.5 %multiply_select_fusion.6 = (f32[1,1024,1024]{1,2,0:T(8,128)}, f32[1,1024,1024]{1,2,0:T(8,128)}, f32[1,1024,1024]{1,2,0:T(8,128)}, f32[1,1024,1024]{1,2,0:T(8,12...) fusion(f32[1,1024,1024]{1,2,0:T(8,128)} %get-tuple-element.465,, ...), kind=kLoop, calls=%fused_computation.154 | loop fusion | flops 25165824 | bytes 67133440 | tf_op jit(solution)/shard_map/transpose(jvp(jit(_where)))/select_n | solution.py:40
  968.9 23.3 %fusion.110 = (bf16[1024,1024]{0,1:T(8,128)(2,1)S(1)}, bf16[1024,1024]{0,1:T(8,128)(2,1)}, bf16[1024,1024]{0,1:T(8,128)(2,1)S(1)}, bf16[1024,1024]{0,1:T(8,128)(2,1)S(1)}) fusion(f32[1,1024,1024]{1,2,0:T(8,128)} %get-tuple-element.464, f32[1024]{0:T(1024)} %bitcast.13, f32[1,1024,1024]{1,2,0:T(8,128)} %get-tuple-element.595, ...), kind=kLoop, calls=%fused_computation.309 | loop fusion | flops 20971520 | bytes 75501568 | tf_op jit(solution)/shard_map/convert.18
  1023.8 8.5 fusion.20
  1032.3 7.0 copy.822
  1050.5 6.9 convolution_convert_fusion.1
  1057.7 6.9 convolution_convert_fusion.3
  1064.6 6.9 convolution_convert_fusion.2
  1071.6 6.9 convolution_convert_fusion
  1101.1 30.0 %all-reduce.109 = (f32[12]{0:T(128)}, f32[12]{0:T(128)}, f32[12]{0:T(128)}) all-reduce(f32[12]{0:T(128)S(1)} %add_add_fusion.9, f32[12]{0:T(128)S(1)} %get-tuple-element.720, f32[12]{0:T(128)S(1)} %get-tuple-element.721), channel_id=1, replica_groups=mesh['dp'=16,'tensor'=2] {'dp'}, use_global_device_ids=true, to_apply=%region_116.118 | all-reduce | flops 36 | bytes 288 | tf_op jit(solution)/shard_map/psum | solution.py:146
  1131.3 30.5 %all-reduce.113 = (bf16[12,64]{1,0:T(8,128)(2,1)S(1)}, bf16[12,64]{1,0:T(8,128)(2,1)S(1)}) all-reduce(bf16[12,64]{1,0:T(8,128)(2,1)S(1)} %convert_element_type.969, bf16[12,64]{1,0:T(8,128)(2,1)S(1)} %convert_element_type.972), channel_id=19, replica_groups=mesh['dp'=16,'tensor'=2] {'dp'}, use_global_device_ids=true, to_apply=%region_109.111.clone | all-reduce | flops 1536 | bytes 6144
  1175.1 61.9 %all-reduce.116.cloned.1.call-done = bf16[768,2,768]{2,1,0:T(2,128)(2,1)} async-done(((bf16[768,2,768]{2,1,0:T(2,128)(2,1)}), bf16[768,2,768]{2,1,0:T(2,128)(2,1)}) %all-reduce.116.cloned.1.call-update) | async-done | bytes 2359312
  1238.7 58.9 %reduce-scatter.50.cloned.1.call-done = bf16[768,48]{0,1:T(8,128)(2,1)} async-done(((bf16[768,768]{0,1:T(8,128)(2,1)}), bf16[768,48]{0,1:T(8,128)(2,1)}) %reduce-scatter.50.cloned.1.call-update) | async-done | bytes 73744 | tf_op jit(solution)/shard_map/reduce_scatter | solution.py:136
  1299.2 25.9 %reduce-scatter.40.cloned.1.call-done = bf16[512,768]{1,0:T(8,128)(2,1)} async-done(((bf16[1024,768]{1,0:T(8,128)(2,1)}), bf16[512,768]{1,0:T(8,128)(2,1)}) %reduce-scatter.40.cloned.1.call-update) | async-done | bytes 786448 | tf_op jit(solution)/shard_map/reduce_scatter | solution.py:315
  1327.8 25.6 %reduce-scatter.32.cloned.1.call-done = bf16[512,768]{1,0:T(8,128)(2,1)} async-done(((bf16[1024,768]{1,0:T(8,128)(2,1)}), bf16[512,768]{1,0:T(8,128)(2,1)}) %reduce-scatter.32.cloned.1.call-update) | async-done | bytes 786448 | tf_op jit(solution)/shard_map/reduce_scatter | solution.py:315
  1356.1 26.2 %reduce-scatter.36.cloned.1.call-done = bf16[512,768]{1,0:T(8,128)(2,1)} async-done(((bf16[1024,768]{1,0:T(8,128)(2,1)}), bf16[512,768]{1,0:T(8,128)(2,1)}) %reduce-scatter.36.cloned.1.call-update) | async-done | bytes 786448 | tf_op jit(solution)/shard_map/reduce_scatter | solution.py:315
  1385.1 25.6 %reduce-scatter.44.cloned.1.call-done = bf16[512,768]{1,0:T(8,128)(2,1)} async-done(((bf16[1024,768]{1,0:T(8,128)(2,1)}), bf16[512,768]{1,0:T(8,128)(2,1)}) %reduce-scatter.44.cloned.1.call-update) | async-done | bytes 786448 | tf_op jit(solution)/shard_map/reduce_scatter | solution.py:315
  1415.7 41.0 %all-reduce.108 = (f32[768]{0:T(1024)S(1)}, f32[256,4]{0,1:T(4,128)S(1)}, f32[256]{0:T(256)S(1)}) all-reduce(f32[768]{0:T(1024)S(1)} %add_add_fusion.7, f32[256,4]{0,1:T(4,128)} %add_add_fusion.4, f32[256]{0:T(256)} %bitcast.1492), channel_id=14, replica_groups=mesh['dp'=16,'tensor'=2] {'dp','tensor'}, use_global_device_ids=true, to_apply=%region_84.86.clone | all-reduce | flops 2048 | bytes 16384
  1468.6 28.4 %reduce-scatter.30.cloned.1.call-done = bf16[512,768]{1,0:T(8,128)(2,1)} async-done(((bf16[1024,768]{1,0:T(8,128)(2,1)}), bf16[512,768]{1,0:T(8,128)(2,1)}) %reduce-scatter.30.cloned.1.call-update) | async-done | bytes 786448 | tf_op jit(solution)/shard_map/reduce_scatter | solution.py:253
  1497.0 28.2 %reduce-scatter.24.cloned.1.call-done = bf16[512,768]{1,0:T(8,128)(2,1)} async-done(((bf16[1024,768]{1,0:T(8,128)(2,1)}), bf16[512,768]{1,0:T(8,128)(2,1)}) %reduce-scatter.24.cloned.1.call-update) | async-done | bytes 786448 | tf_op jit(solution)/shard_map/reduce_scatter | solution.py:253
  1532.2 94.9 %reduce-scatter.48.cloned.1.call-done = f32[24,256]{1,0:T(8,128)} async-done(((f32[768,256]{1,0:T(8,128)}), f32[24,256]{1,0:T(8,128)}) %reduce-scatter.48.cloned.1.call-update) | async-done | bytes 24592 | tf_op jit(solution)/shard_map/reduce_scatter | solution.py:141
  (1491 shorter events, 601.6 us)
Async XLA Ops:
  7.2 313.6 %all-gather.25.cloned.1.call-start = ((), (), s32[]{:S(2)}) async-start(), calls=%async_computation.24 | async-start | bytes 2359296 | tf_op jit(solution)/shard_map/all_gather | solution.py:211
  56.0 266.9 %all-gather.23.cloned.1.call-start = ((), (), s32[]{:S(2)}) async-start(), calls=%async_computation.22 | async-start | bytes 2359296 | tf_op jit(solution)/shard_map/all_gather | solution.py:211
  56.7 269.5 %all-gather.21.cloned.1.call-start = ((), (), s32[]{:S(2)}) async-start(), calls=%async_computation.20 | async-start | bytes 2359296 | tf_op jit(solution)/shard_map/all_gather | solution.py:211
  57.5 271.9 %all-gather.15.cloned.1.call-start = ((), (), s32[]{:S(2)}) async-start(), calls=%async_computation.16 | async-start | bytes 2359296 | tf_op jit(solution)/shard_map/all_gather | solution.py:211
  58.0 274.3 %all-gather.27.cloned.1.call-start = ((), (), s32[]{:S(2)}) async-start(), calls=%async_computation.26 | async-start | bytes 2359296 | tf_op jit(solution)/shard_map/all_gather | solution.py:265
  65.9 105.8 %copy-start.476 = (bf16[12,4]{0,1:T(4,128)(2,1)S(1)}, bf16[12,4]{0,1:T(4,128)(2,1)}, u32[]{:S(2)}) copy-start(bf16[12,4]{0,1:T(4,128)(2,1)} %param.24) | copy-start | bytes 292
  65.9 123.2 %copy-start.460 = (bf16[12,16]{1,0:T(8,128)(2,1)S(1)}, bf16[12,16]{1,0:T(8,128)(2,1)}, u32[]{:S(2)}) copy-start(bf16[12,16]{1,0:T(8,128)(2,1)} %param.23) | copy-start | bytes 1156
  65.9 143.2 %copy-start.477 = (bf16[8,4]{0,1:T(4,128)(2,1)S(1)}, bf16[8,4]{0,1:T(4,128)(2,1)}, u32[]{:S(2)}) copy-start(bf16[8,4]{0,1:T(4,128)(2,1)} %param.25) | copy-start | bytes 196
  65.9 209.4 %copy-start.487 = (bf16[12]{0:T(256)(128)(2,1)S(1)}, bf16[12]{0:T(256)(128)(2,1)}, u32[]{:S(2)}) copy-start(bf16[12]{0:T(256)(128)(2,1)} %param.27) | copy-start | bytes 76
  66.0 209.4 %copy-start.484 = (bf16[12]{0:T(256)(128)(2,1)S(1)}, bf16[12]{0:T(256)(128)(2,1)}, u32[]{:S(2)}) copy-start(bf16[12]{0:T(256)(128)(2,1)} %param.28) | copy-start | bytes 76
  66.0 235.4 %copy-start.483 = (bf16[12]{0:T(256)(128)(2,1)S(1)}, bf16[12]{0:T(256)(128)(2,1)}, u32[]{:S(2)}) copy-start(bf16[12]{0:T(256)(128)(2,1)} %param.29) | copy-start | bytes 76
  66.0 236.2 %copy-start.478 = (bf16[12,4]{0,1:T(4,128)(2,1)S(1)}, bf16[12,4]{0,1:T(4,128)(2,1)}, u32[]{:S(2)}) copy-start(bf16[12,4]{0,1:T(4,128)(2,1)} %param.30) | copy-start | bytes 292
  66.0 266.3 %all-gather.19.cloned.1.call-start = ((), (), s32[]{:S(2)}) async-start(), calls=%async_computation.18 | async-start | bytes 1253376 | tf_op jit(solution)/shard_map/all_gather | solution.py:174
  66.6 270.7 %all-gather.29.cloned.1.call-start = ((), (), s32[]{:S(2)}) async-start(), calls=%async_computation.29 | async-start | bytes 2359296 | tf_op jit(solution)/shard_map/all_gather | solution.py:265
  67.3 274.5 %all-gather.33.cloned.1.call-start = ((), (), s32[]{:S(2)}) async-start(), calls=%async_computation.35 | async-start | bytes 2359296 | tf_op jit(solution)/shard_map/all_gather | solution.py:265
  68.1 278.3 %all-gather.17.cloned.1.call-start = ((), (), s32[]{:S(2)}) async-start(), calls=%async_computation.17 | async-start | bytes 2506752 | tf_op jit(solution)/shard_map/all_gather | solution.py:169
  68.8 517.5 %all-gather.31.cloned.1.call-start = ((), (), s32[]{:S(2)}) async-start(), calls=%async_computation.32 | async-start | bytes 2359296 | tf_op jit(solution)/shard_map/all_gather | solution.py:265
  69.4 1095.1 %reduce-scatter.54.cloned.1.call-start = ((), (), s32[]{:S(2)}) async-start(), calls=%async_computation.41 | async-start | bytes 69632
  104.6 280.1 %copy-start.296 = (bf16[16,48,12]{2,1,0:T(8,128)(2,1)}, bf16[16,48,12]{2,1,0:T(8,128)(2,1)S(1)}, u32[]{:S(2)}) copy-start(bf16[16,48,12]{2,1,0:T(8,128)(2,1)S(1)} %copy.866) | copy-start | bytes 55300
  171.6 157.7 %copy-start.47 = (bf16[768,256]{1,0:T(8,128)(2,1)}, bf16[768,256]{1,0:T(8,128)(2,1)S(1)}, u32[]{:S(2)}) copy-start(bf16[768,256]{1,0:T(8,128)(2,1)S(1)} %all_gather.60) | copy-start | bytes 1179652
  171.7 184.5 %copy-start.373 = (pred[1024]{0:T(1024)(128)(4,1)}, pred[1024]{0:T(1024)(128)(4,1)S(1)}, u32[]{:S(2)}) copy-start(pred[1024]{0:T(1024)(128)(4,1)S(1)} %get-tuple-element.421) | copy-start | bytes 3076
  171.7 184.5 %copy-start.375 = (pred[1024]{0:T(1024)(128)(4,1)}, pred[1024]{0:T(1024)(128)(4,1)S(1)}, u32[]{:S(2)}) copy-start(pred[1024]{0:T(1024)(128)(4,1)S(1)} %get-tuple-element.422) | copy-start | bytes 3076
  171.7 184.5 %copy-start.377 = (pred[1024]{0:T(1024)(128)(4,1)}, pred[1024]{0:T(1024)(128)(4,1)S(1)}, u32[]{:S(2)}) copy-start(pred[1024]{0:T(1024)(128)(4,1)S(1)} %get-tuple-element.423) | copy-start | bytes 3076
  275.3 116.0 %copy-start.464 = (f32[12]{0:T(128)}, f32[12]{0:T(128)S(1)}, u32[]{:S(2)}) copy-start(f32[12]{0:T(128)S(1)} %convert_element_type.839) | copy-start | bytes 148
  275.4 116.0 %copy-start.466 = (f32[12]{0:T(128)}, f32[12]{0:T(128)S(1)}, u32[]{:S(2)}) copy-start(f32[12]{0:T(128)S(1)} %fusion.533) | copy-start | bytes 148
  283.3 145.1 %copy-start.379 = (pred[1024]{0:T(1024)(128)(4,1)}, pred[1024]{0:T(1024)(128)(4,1)S(1)}, u32[]{:S(2)}) copy-start(pred[1024]{0:T(1024)(128)(4,1)S(1)} %get-tuple-element.418) | copy-start | bytes 3076
  283.3 145.1 %copy-start.382 = (pred[1024]{0:T(1024)(128)(4,1)}, pred[1024]{0:T(1024)(128)(4,1)S(1)}, u32[]{:S(2)}) copy-start(pred[1024]{0:T(1024)(128)(4,1)S(1)} %get-tuple-element.419) | copy-start | bytes 3076
  393.7 91.6 %copy-start.215 = (f32[1024,12]{0,1:T(8,128)}, f32[1024,12]{0,1:T(8,128)S(1)}, u32[]{:S(2)}) copy-start(f32[1024,12]{0,1:T(8,128)S(1)} %get-tuple-element.665) | copy-start | bytes 147460
  572.6 116.0 %copy-start = (f32[1024,768]{0,1:T(8,128)}, f32[1024,768]{0,1:T(8,128)S(1)}, u32[]{:S(2)}) copy-start(f32[1024,768]{0,1:T(8,128)S(1)} %get-tuple-element.630) | copy-start | bytes 9437188
  944.3 221.6 %reduce-scatter.52.cloned.1.call-start = ((), (), s32[]{:S(2)}) async-start(), calls=%async_computation.40 | async-start | bytes 208896
  1015.9 151.4 %reduce-scatter.34.cloned.1.call-start = ((), (), s32[]{:S(2)}) async-start(), calls=%async_computation.28 | async-start | bytes 786432 | tf_op jit(solution)/shard_map/reduce_scatter | solution.py:318
  1017.8 151.8 %reduce-scatter.38.cloned.1.call-start = ((), (), s32[]{:S(2)}) async-start(), calls=%async_computation.31 | async-start | bytes 786432 | tf_op jit(solution)/shard_map/reduce_scatter | solution.py:318
  1019.8 151.5 %reduce-scatter.42.cloned.1.call-start = ((), (), s32[]{:S(2)}) async-start(), calls=%async_computation.34 | async-start | bytes 786432 | tf_op jit(solution)/shard_map/reduce_scatter | solution.py:318
  1021.8 151.0 %reduce-scatter.46.cloned.1.call-start = ((), (), s32[]{:S(2)}) async-start(), calls=%async_computation.37 | async-start | bytes 786432 | tf_op jit(solution)/shard_map/reduce_scatter | solution.py:318
  1023.7 213.3 %all-reduce.116.cloned.1.call-start = ((), (), s32[]{:S(2)}) async-start(), calls=%async_computation.42 | async-start | bytes 4718592
  1039.3 258.3 %reduce-scatter.50.cloned.1.call-start = ((), (), s32[]{:S(2)}) async-start(), calls=%async_computation.39 | async-start | bytes 1253376 | tf_op jit(solution)/shard_map/reduce_scatter | solution.py:136
  1050.5 274.5 %reduce-scatter.40.cloned.1.call-start = ((), (), s32[]{:S(2)}) async-start(), calls=%async_computation.33 | async-start | bytes 2359296 | tf_op jit(solution)/shard_map/reduce_scatter | solution.py:315
  1057.4 295.9 %reduce-scatter.32.cloned.1.call-start = ((), (), s32[]{:S(2)}) async-start(), calls=%async_computation.27 | async-start | bytes 2359296 | tf_op jit(solution)/shard_map/reduce_scatter | solution.py:315
  1064.6 317.7 %reduce-scatter.36.cloned.1.call-start = ((), (), s32[]{:S(2)}) async-start(), calls=%async_computation.30 | async-start | bytes 2359296 | tf_op jit(solution)/shard_map/reduce_scatter | solution.py:315
  1071.5 339.2 %reduce-scatter.44.cloned.1.call-start = ((), (), s32[]{:S(2)}) async-start(), calls=%async_computation.36 | async-start | bytes 2359296 | tf_op jit(solution)/shard_map/reduce_scatter | solution.py:315
  1078.4 378.3 %reduce-scatter.28.cloned.1.call-start = ((), (), s32[]{:S(2)}) async-start(), calls=%async_computation.23 | async-start | bytes 2359296 | tf_op jit(solution)/shard_map/reduce_scatter | solution.py:253
  1083.5 385.0 %reduce-scatter.26.cloned.1.call-start = ((), (), s32[]{:S(2)}) async-start(), calls=%async_computation.21 | async-start | bytes 2359296 | tf_op jit(solution)/shard_map/reduce_scatter | solution.py:253
  1088.6 408.4 %reduce-scatter.30.cloned.1.call-start = ((), (), s32[]{:S(2)}) async-start(), calls=%async_computation.25 | async-start | bytes 2359296 | tf_op jit(solution)/shard_map/reduce_scatter | solution.py:253
  1093.3 432.0 %reduce-scatter.24.cloned.1.call-start = ((), (), s32[]{:S(2)}) async-start(), calls=%async_computation.19 | async-start | bytes 2359296 | tf_op jit(solution)/shard_map/reduce_scatter | solution.py:253
  1098.4 528.7 %reduce-scatter.48.cloned.1.call-start = ((), (), s32[]{:S(2)}) async-start(), calls=%async_computation.38 | async-start | bytes 811008 | tf_op jit(solution)/shard_map/reduce_scatter | solution.py:141
  1171.3 153.8 %copy-start.48 = (bf16[768,256]{1,0:T(8,128)(2,1)S(1)}, bf16[768,256]{1,0:T(8,128)(2,1)}, u32[]{:S(2)}) copy-start(bf16[768,256]{1,0:T(8,128)(2,1)} %copy-done.47) | copy-start | bytes 1179652
  1172.7 152.3 %copy-start.224 = (bf16[512,256]{0,1:T(8,128)(2,1)S(1)}, bf16[512,256]{0,1:T(8,128)(2,1)}, u32[]{:S(2)}) copy-start(bf16[512,256]{0,1:T(8,128)(2,1)} %reduce-scatter.42.cloned.1.call-done) | copy-start | bytes 786436
  1327.8 83.0 %copy-start.354 = (f32[512]{0:T(512)S(1)}, f32[512]{0:T(512)}, u32[]{:S(2)}) copy-start(f32[512]{0:T(512)} %copy-done.353) | copy-start | bytes 6148
  (472 other events, 4422.9 us)
Sparse Core Ops, SparseCore 0:
  56.1 26.9 all-gather.24
  84.7 28.0 all-gather.22
  114.4 29.8 all-gather.20
  145.6 28.7 all-gather.14
  176.4 27.0 all-gather.26
  205.6 38.2 all-gather.18
  246.0 26.2 all-gather.28
  273.9 27.1 all-gather.32
  303.4 42.3 all-gather.16
  347.1 25.8 all-gather.30
  944.4 49.6 reduce-scatter.53
  1016.0 51.2 reduce-scatter.51
  1069.5 13.6 reduce-scatter.33
  1085.3 14.6 reduce-scatter.37
  1102.1 14.6 reduce-scatter.41
  1118.9 14.6 reduce-scatter.45
  1137.5 99.4 all-reduce.115
  1240.5 57.1 reduce-scatter.49
  1299.8 25.1 reduce-scatter.39
  1327.1 26.1 reduce-scatter.31
  1356.1 26.1 reduce-scatter.35
  1384.6 26.1 reduce-scatter.43
  1413.0 26.8 reduce-scatter.27
  1442.0 26.5 reduce-scatter.25
  1470.8 26.1 reduce-scatter.29
  1499.1 26.1 reduce-scatter.23
  1530.8 96.2 reduce-scatter.47
where the time goes:
time: 1640 us; the launch traced here: 1630 us
  waiting for transfers between devices  386 us (24%)
  blocking collectives  369 us (22%)
  matrix products  355 us (22%)
  other arithmetic  296 us (18%)
  local copies, waits for them, and re-layouts  206 us (13%)
  between operations  22.3 us (1%)
    unnamed x3, blocking collectives  114 us
    reduce_scatter x4, waiting for transfers between devices, local(): lax.psum_scatter(back_lowered.astype(jnp.bfloat16), 'tensor', scatter_dim...  103 us
    reduce_scatter x1, waiting for transfers between devices, reduce_gradients(): lax.psum_scatter(shared_terms[0], ('dp', 'tensor'), scatter_dimension=0,...  94.9 us
    unnamed x1029, local copies, waits for them, and re-layouts  77.2 us
    unnamed x30, waiting for transfers between devices  67.2 us
    all_gather x1, blocking collectives, local(): lax.all_gather(selection, ('dp', 'tensor'), axis=0, tiled=True)  67 us
    all_gather x1, blocking collectives, local(): lax.all_gather(stencil, ('dp', 'tensor'), axis=0, tiled=True)  65.5 us
    reduce_scatter x4, waiting for transfers between devices, local(): lax.psum_scatter(jnp.dot(lifted_low, readout_full, preferred_element_type...  61.5 us
  transfers between devices with their start and end apart: 27, of which 10 were waited for; matrix products, arithmetic and copies ran while one was open for 29% of the time, Pallas kernels for 0%

commit v1 on v0

v1 whole, which is shorter than its diff:
```python
import functools

import jax
import jax.numpy as jnp
from jax import lax
from jax.experimental import pallas as pl
from jax.experimental.pallas import tpu as pltpu
from jax.sharding import PartitionSpec as P

WIDTH = 768
HEADS = 24
HEAD_DIM = 64
STATE = 128
TAPS = 4
INNER = 1536
SLOT = 1024
CHUNK = 128
LANES = 128
GROUP = 256
CHANNELS = INNER + 2 * STATE
EPS = 1e-05
BF = jnp.bfloat16
F32 = jnp.float32
VMEM_LIMIT = 56 * 1024 * 1024


def nn(a, b):
    return lax.dot_general(a, b, (((1,), (0,)), ((), ())), preferred_element_type=F32)


def nt(a, b):
    return lax.dot_general(a, b, (((1,), (1,)), ((), ())), preferred_element_type=F32)


def tn(a, b):
    return lax.dot_general(a, b, (((0,), (0,)), ((), ())), preferred_element_type=F32)


def exact_dot(a, b):
    return lax.dot_general(
        a, b, (((1,), (0,)), ((), ())), preferred_element_type=F32, precision=lax.Precision.HIGHEST
    )


def pieces(v):
    high = v.astype(BF)
    low = (v - high.astype(F32)).astype(BF)
    return high, low


def doubled(v):
    high, low = pieces(v)
    return (high.astype(F32) + pltpu.roll(low.astype(F32), HEADS, 1)).astype(BF)


def softplus(v):
    return jnp.maximum(v, 0.0) + jnp.log1p(jnp.exp(-jnp.abs(v)))


def sigmoid(v):
    return 1.0 / (1.0 + jnp.exp(-v))


def wide(column):
    return jnp.broadcast_to(column, (CHUNK, LANES))


def shifted(block, tail):
    full = jnp.concatenate([tail, block], axis=0)
    return [pltpu.roll(full, back, 0)[8:] for back in range(1, TAPS)]


def total_of(block, moved, masks, taps_ref, lanes):
    total = taps_ref[TAPS : TAPS + 1, lanes] + block * taps_ref[TAPS - 1 : TAPS, lanes]
    masked = [moved[back - 1] * masks[back - 1] for back in range(1, TAPS)]
    for back in range(1, TAPS):
        total = total + masked[back - 1] * taps_ref[TAPS - 1 - back : TAPS - back, lanes]
    return total, masked


def order_masks():
    row = lax.broadcasted_iota(jnp.int32, (CHUNK, CHUNK), 0)
    column = lax.broadcasted_iota(jnp.int32, (CHUNK, CHUNK), 1)
    return row, column


def rates(sraw_ref, heads_ref):
    lane = lax.broadcasted_iota(jnp.int32, (CHUNK, LANES), 1)
    raw = sraw_ref[...] + heads_ref[0:1, :]
    step = jnp.where(lane < HEADS, softplus(raw), 0.0)
    rate = step * heads_ref[1:2, :]
    row, column = order_masks()
    lower = (row >= column).astype(F32)
    cumulative = exact_dot(lower, rate)
    return raw, step, rate, cumulative


def factors(cumulative, cols_ref):
    lane = lax.broadcasted_iota(jnp.int32, (CHUNK, LANES), 1)
    keep = lane < HEADS
    last = cumulative[CHUNK - 1 : CHUNK, :]
    stay = jnp.where(keep, jnp.exp(last - cumulative) * cols_ref[:, 4:5], 0.0)
    come = jnp.where(keep, jnp.exp(cumulative) * cols_ref[:, 3:4], 0.0)
    return stay, come


def pair_of(block):
    lane = lax.broadcasted_iota(jnp.int32, block.shape, 1)
    zero = jnp.zeros_like(block)
    return jnp.concatenate(
        [jnp.where(lane < HEAD_DIM, block, zero), jnp.where(lane >= HEAD_DIM, block, zero)], axis=0
    )


def scan_forward(
    x_ref,
    tail_ref,
    sraw_ref,
    cols_ref,
    segrow_ref,
    taps_ref,
    heads_ref,
    spread_ref,
    core_ref,
    conv_ref,
    maps_ref,
    reach_ref,
    state_ref,
    decay_ref,
    carry,
    run,
):
    chunk = pl.program_id(1)

    @pl.when(chunk == 0)
    def _():
        carry[...] = jnp.zeros_like(carry)
        run[...] = jnp.zeros_like(run)

    masks = [wide(cols_ref[:, k : k + 1]) for k in range(TAPS - 1)]
    _, step, rate, cumulative = rates(sraw_ref, heads_ref)
    stay, come = factors(cumulative, cols_ref)
    lane = lax.broadcasted_iota(jnp.int32, (CHUNK, LANES), 1)
    whole = cumulative + run[0:1, :]
    reach = jnp.where(lane < HEADS, jnp.exp(whole) * cols_ref[:, 7:8], 0.0)
    reach_ref[...] = reach
    run[...] = jnp.broadcast_to(whole[CHUNK - 1 : CHUNK, :], run.shape)
    decay_ref[0, 0] = nn(doubled(jnp.broadcast_to(reach[CHUNK - 1 : CHUNK, :], (16, LANES))), spread_ref[...])[:8]

    maps = []
    for part in range(2):
        lanes = slice(INNER + part * STATE, INNER + (part + 1) * STATE)
        block = x_ref[:, lanes].astype(F32)
        total, _ = total_of(block, shifted(block, tail_ref[0, :, lanes].astype(F32)), masks, taps_ref, lanes)
        maps.append((total * sigmoid(total)).astype(BF))
        maps_ref[:, part * STATE : (part + 1) * STATE] = maps[part]
    entry, reader = maps
    row, column = order_masks()
    same = (row >= column) & (wide(cols_ref[:, 5:6]) == segrow_ref[0, 0:1, :])
    inner = jnp.where(same, nt(reader, entry), 0.0)
    entry_t = jnp.transpose(entry.astype(F32)).astype(BF)
    cum_t = jnp.transpose(cumulative)
    step2, stay2, come2 = doubled(step), doubled(stay), doubled(come)

    for group in range(INNER // GROUP):
        span = slice(group * GROUP, (group + 1) * GROUP)
        step_x = nn(step2, spread_ref[:, span])
        stay_x = nn(stay2, spread_ref[:, span])
        come_x = nn(come2, spread_ref[:, span])
        old = carry[:, span]
        brought = nn(reader, old.astype(BF)) * come_x
        kept = []
        for half in range(GROUP // LANES):
            lanes = slice(group * GROUP + half * LANES, group * GROUP + (half + 1) * LANES)
            local = slice(half * LANES, (half + 1) * LANES)
            block = x_ref[:, lanes].astype(F32)
            total, _ = total_of(block, shifted(block, tail_ref[0, :, lanes].astype(F32)), masks, taps_ref, lanes)
            convolved = total * sigmoid(total)
            conv_ref[:, lanes] = convolved.astype(BF)
            scaled = (convolved * step_x[:, local]).astype(BF)
            kept.append((scaled.astype(F32) * stay_x[:, local]).astype(BF))
            weights = []
            for head in (group * 4 + half * 2, group * 4 + half * 2 + 1):
                gap = wide(cumulative[:, head : head + 1]) - cum_t[head : head + 1, :]
                weights.append((inner * jnp.exp(jnp.minimum(gap, 0.0))).astype(BF))
            diagonal = nn(jnp.concatenate(weights, axis=1), pair_of(scaled))
            core_ref[:, lanes] = diagonal + brought[:, local]
        fresh = nn(entry_t, jnp.concatenate(kept, axis=1))
        fresh = old * come_x[CHUNK - 1 : CHUNK, :] + fresh
        carry[:, span] = fresh
        state_ref[0, 0, :, span] = fresh.astype(BF)


def scan_backward(
    x_ref,
    tail_ref,
    sraw_ref,
    cols_ref,
    segrow_ref,
    taps_ref,
    heads_ref,
    spread_ref,
    gather_ref,
    out_ref,
    rows_ref,
    state_ref,
    decay_ref,
    enter_ref,
    back_ref,
    grad_ref,
    raw_ref,
    halo_ref,
    acc_ref,
    head_acc_ref,
    carry,
    later,
):
    micro = pl.program_id(0)
    chunk = pl.num_programs(1) - 1 - pl.program_id(1)

    @pl.when((micro == 0) & (pl.program_id(1) == 0))
    def _():
        acc_ref[...] = jnp.zeros_like(acc_ref)
        head_acc_ref[...] = jnp.zeros_like(head_acc_ref)

    first = pl.program_id(1) == 0
    start = chunk == 0
    gather = gather_ref[...]

    @pl.when(first)
    def _():
        later[...] = jnp.zeros_like(later)
        carry[...] = back_ref[0].astype(F32)

    masks = [wide(cols_ref[:, k : k + 1]) for k in range(TAPS - 1)]
    raw, step, rate, cumulative = rates(sraw_ref, heads_ref)
    stay, come = factors(cumulative, cols_ref)

    maps = []
    for part in range(2):
        lanes = slice(INNER + part * STATE, INNER + (part + 1) * STATE)
        block = x_ref[:, lanes].astype(F32)
        moved = shifted(block, tail_ref[0, :, lanes].astype(F32))
        total, masked = total_of(block, moved, masks, taps_ref, lanes)
        gate = sigmoid(total)
        maps.append(((total * gate).astype(BF), gate * (1.0 + total * (1.0 - gate)), block, masked))
    entry, reader = maps[0][0], maps[1][0]
    row, column = order_masks()
    same = (row >= column) & (wide(cols_ref[:, 5:6]) == segrow_ref[0, 0:1, :])
    inner = jnp.where(same, nt(reader, entry), 0.0)
    reader_t = jnp.transpose(reader.astype(F32)).astype(BF)
    cum_t = jnp.transpose(cumulative)
    step2, stay2, come2 = doubled(step), doubled(stay), doubled(come)

    back_inner = jnp.zeros((CHUNK, CHUNK), F32)
    back_entry = jnp.zeros((CHUNK, STATE), F32)
    back_reader = jnp.zeros((CHUNK, STATE), F32)
    columns = jnp.zeros((CHUNK, LANES), F32)
    steps = jnp.zeros((CHUNK, LANES), F32)
    products = []

    def conv_back(back_total, block, masked, lanes):
        parts = [back_total * block] + [back_total * value for value in masked]
        for index, value in enumerate([back_total] + parts):
            acc_ref[index * 8 : index * 8 + 8, lanes] += jnp.sum(value.reshape(CHUNK // 8, 8, LANES), axis=0)
        result = back_total * taps_ref[TAPS - 1 : TAPS, lanes]
        edge = jnp.zeros((8, LANES), F32)
        for back in range(1, TAPS):
            held = back_total * masks[back - 1]
            full = jnp.concatenate([held, later[back - 1, :, lanes]], axis=0)
            tap = taps_ref[TAPS - 1 - back : TAPS - back, lanes]
            result = result + pltpu.roll(full, CHUNK + 8 - back, 0)[:CHUNK] * tap
            head = jnp.concatenate([jnp.zeros((8, LANES), F32), held[:8]], axis=0)
            edge = edge + pltpu.roll(head, 16 - back, 0)[:8] * tap
            later[back - 1, :, lanes] = held[:8]
        grad_ref[:, lanes] = result.astype(BF)
        halo_ref[0, :, lanes] = edge.astype(BF)

    for group in range(INNER // GROUP):
        span = slice(group * GROUP, (group + 1) * GROUP)
        step_x = nn(step2, spread_ref[:, span])
        stay_x = nn(stay2, spread_ref[:, span])
        come_x = nn(come2, spread_ref[:, span])
        back_carry = carry[:, span]
        back_low = back_carry.astype(BF)
        from_state = nn(entry, back_low) * stay_x
        out = out_ref[:, span]
        out_f = out.astype(F32)
        come_out = (out_f * come_x).astype(BF)
        enter = enter_ref[0, :, span].astype(F32)
        before = jnp.where(
            start, enter, state_ref[0, 0, :, span].astype(F32) + enter * decay_ref[0, 0, 0:1, span]
        )
        back_reader = back_reader + nt(come_out, before.astype(BF))
        kept = []
        within = []
        for half in range(GROUP // LANES):
            lanes = slice(group * GROUP + half * LANES, group * GROUP + (half + 1) * LANES)
            local = slice(half * LANES, (half + 1) * LANES)
            block = x_ref[:, lanes].astype(F32)
            moved = shifted(block, tail_ref[0, :, lanes].astype(F32))
            total, masked = total_of(block, moved, masks, taps_ref, lanes)
            gate = sigmoid(total)
            convolved = total * gate
            slope = gate * (1.0 + total * (1.0 - gate))
            scaled = (convolved * step_x[:, local]).astype(BF)
            scaled_f = scaled.astype(F32)
            kept.append((scaled_f * stay_x[:, local]).astype(BF))
            within.append(jnp.sum(scaled_f * from_state[:, local], axis=0, keepdims=True))
            back_pair = nt(out[:, local], pair_of(scaled))
            weights = []
            for index in range(2):
                head = group * 4 + half * 2 + index
                gap = wide(cumulative[:, head : head + 1]) - cum_t[head : head + 1, :]
                table = jnp.exp(jnp.minimum(gap, 0.0))
                weights.append((inner * table).astype(BF))
                back_inner = back_inner + back_pair[:, index * CHUNK : (index + 1) * CHUNK] * table
            back_scaled = tn(jnp.concatenate(weights, axis=0), pair_of(out[:, local])) + from_state[:, local]
            high, low = pieces(scaled_f * back_scaled)
            columns = columns + nn(high, gather[lanes, :]) + nn(low, gather[lanes, :])
            steps = steps + nn((convolved * back_scaled).astype(BF), gather[lanes, :])
            back_convolved = out_f[:, local] * taps_ref[5:6, lanes] + back_scaled * step_x[:, local]
            conv_back(back_convolved * slope, block, masked, lanes)
        back_entry = back_entry + nt(jnp.concatenate(kept, axis=1), back_low)
        decayed = back_carry * come_x[CHUNK - 1 : CHUNK, :]
        carry[:, span] = decayed + nn(reader_t, come_out)
        products.append(jnp.sum(decayed * before, axis=0, keepdims=True) + jnp.concatenate(within, axis=1))

    back_inner = jnp.where(same, back_inner, 0.0).astype(BF)
    back_reader = back_reader + nn(back_inner, entry)
    back_entry = back_entry + tn(back_inner, reader)
    for part, value in ((0, back_entry), (1, back_reader)):
        lanes = slice(INNER + part * STATE, INNER + (part + 1) * STATE)
        conv_back(value * maps[part][1], maps[part][2], maps[part][3], lanes)

    high, low = pieces(jnp.broadcast_to(jnp.concatenate(products, axis=1), (16, INNER)))
    gamma = nn(high, gather) + nn(low, gather)
    ends = jnp.where(row[:, :LANES] == CHUNK - 1, gamma[0:1, :], 0.0)
    back_cumulative = rows_ref[...] - columns + ends
    upper = (row <= column).astype(F32)
    back_rate = exact_dot(upper, back_cumulative)
    back_step = steps + back_rate * heads_ref[1:2, :]
    back_raw = back_step * sigmoid(raw)
    raw_ref[...] = back_raw.astype(BF)
    head_acc_ref[0:8, :] += jnp.sum(back_raw.reshape(CHUNK // 8, 8, LANES), axis=0)
    head_acc_ref[8:16, :] += jnp.sum((back_rate * rate).reshape(CHUNK // 8, 8, LANES), axis=0)


def constant(shape):
    return pl.BlockSpec(shape, lambda m, c: (0,) * len(shape))


def run_forward(x, tails, sraw, cols, segrow, taps, heads, spread, chunks):
    rows = x.shape[0]
    micro = rows // (chunks * CHUNK)
    flat = lambda width: pl.BlockSpec((CHUNK, width), lambda m, c: (m * chunks + c, 0))
    return pl.pallas_call(
        scan_forward,
        grid=(micro, chunks),
        in_specs=[
            flat(CHANNELS),
            pl.BlockSpec((1, 8, CHANNELS), lambda m, c: (m * chunks + c, 0, 0)),
            flat(LANES),
            flat(LANES),
            pl.BlockSpec((1, 8, LANES), lambda m, c: (m * chunks + c, 0, 0)),
            constant((8, CHANNELS)),
            constant((8, LANES)),
            constant((LANES, INNER)),
        ],
        out_specs=[
            flat(INNER),
            flat(INNER),
            flat(2 * STATE),
            flat(LANES),
            pl.BlockSpec((1, 1, STATE, INNER), lambda m, c: (m, c, 0, 0)),
            pl.BlockSpec((1, 1, 8, INNER), lambda m, c: (m, c, 0, 0)),
        ],
        out_shape=[
            jax.ShapeDtypeStruct((rows, INNER), F32),
            jax.ShapeDtypeStruct((rows, INNER), BF),
            jax.ShapeDtypeStruct((rows, 2 * STATE), BF),
            jax.ShapeDtypeStruct((rows, LANES), F32),
            jax.ShapeDtypeStruct((micro, chunks, STATE, INNER), BF),
            jax.ShapeDtypeStruct((micro, chunks, 8, INNER), F32),
        ],
        scratch_shapes=[pltpu.VMEM((STATE, INNER), F32), pltpu.VMEM((8, LANES), F32)],
        compiler_params=pltpu.CompilerParams(vmem_limit_bytes=VMEM_LIMIT),
        name="scan_forward",
    )(x, tails, sraw, cols, segrow, taps, heads, spread)


def run_backward(x, tails, sraw, cols, segrow, taps, heads, spread, gather, out, row_sums, states, decay, enter, back, chunks):
    rows = x.shape[0]
    micro = rows // (chunks * CHUNK)
    place = lambda m, c: m * chunks + chunks - 1 - c
    flat = lambda width: pl.BlockSpec((CHUNK, width), lambda m, c: (place(m, c), 0))
    return pl.pallas_call(
        scan_backward,
        grid=(micro, chunks),
        in_specs=[
            flat(CHANNELS),
            pl.BlockSpec((1, 8, CHANNELS), lambda m, c: (place(m, c), 0, 0)),
            flat(LANES),
            flat(LANES),
            pl.BlockSpec((1, 8, LANES), lambda m, c: (place(m, c), 0, 0)),
            constant((8, CHANNELS)),
            constant((8, LANES)),
            constant((LANES, INNER)),
            constant((INNER, LANES)),
            flat(INNER),
            flat(LANES),
            pl.BlockSpec((1, 1, STATE, INNER), lambda m, c: (m, jnp.maximum(chunks - 2 - c, 0), 0, 0)),
            pl.BlockSpec((1, 1, 8, INNER), lambda m, c: (m, jnp.maximum(chunks - 2 - c, 0), 0, 0)),
            pl.BlockSpec((1, STATE, INNER), lambda m, c: (m, 0, 0)),
            pl.BlockSpec((1, STATE, INNER), lambda m, c: (m, 0, 0)),
        ],
        out_specs=[
            flat(CHANNELS),
            flat(LANES),
            pl.BlockSpec((1, 8, CHANNELS), lambda m, c: (m, 0, 0)),
            constant((40, CHANNELS)),
            constant((16, LANES)),
        ],
        out_shape=[
            jax.ShapeDtypeStruct((rows, CHANNELS), BF),
            jax.ShapeDtypeStruct((rows, LANES), BF),
            jax.ShapeDtypeStruct((micro, 8, CHANNELS), BF),
            jax.ShapeDtypeStruct((40, CHANNELS), F32),
            jax.ShapeDtypeStruct((16, LANES), F32),
        ],
        scratch_shapes=[
            pltpu.VMEM((STATE, INNER), F32),
            pltpu.VMEM((TAPS - 1, 8, CHANNELS), F32),
        ],
        compiler_params=pltpu.CompilerParams(vmem_limit_bytes=VMEM_LIMIT),
        name="scan_backward",
    )(x, tails, sraw, cols, segrow, taps, heads, spread, gather, out, row_sums, states, decay, enter, back)


def gather_weights(shards):
    flat = jnp.concatenate([shard.reshape(-1) for shard in shards])
    everyone = lax.all_gather(flat, ("dp", "tensor"), axis=0, tiled=False)
    everyone = everyone.reshape(lax.axis_size("dp"), lax.axis_size("tensor"), flat.shape[0])
    result = []
    start = 0
    for shard in shards:
        result.append(everyone[:, :, start : start + shard.size].reshape(everyone.shape[:2] + shard.shape))
        start += shard.size
    return result


def join(shards, dp_dim, tensor_dim):
    groups, members = shards.shape[:2]
    shape = list(shards.shape[2:])
    order = []
    for dim in range(len(shape)):
        if dim == dp_dim:
            order.append(0)
        if dim == tensor_dim:
            order.append(1)
        order.append(dim + 2)
    full = shape[:]
    full[dp_dim] *= groups
    full[tensor_dim] *= members
    return jnp.transpose(shards, order).reshape(full)


def cut(full, dp_dim, tensor_dim):
    groups, members = lax.axis_size("dp"), lax.axis_size("tensor")
    shape = []
    for dim, size in enumerate(full.shape):
        if dim == dp_dim:
            shape.append(groups)
            size //= groups
        if dim == tensor_dim:
            shape.append(members)
            size //= members
        shape.append(size)
    both = full.reshape(shape)
    position = dp_dim + (1 if tensor_dim < dp_dim else 0)
    where = tensor_dim + (1 if dp_dim <= tensor_dim else 0)
    return jnp.moveaxis(both, (position, where), (0, 1))


def reduce_shards(grads, places, shapes):
    groups, members = lax.axis_size("dp"), lax.axis_size("tensor")
    flat = jnp.concatenate(
        [cut(grad.astype(BF), *place).reshape(groups * members, -1) for grad, place in zip(grads, places)], axis=1
    )
    mine = lax.psum_scatter(flat, ("dp", "tensor"), scatter_dimension=0, tiled=True).reshape(-1).astype(F32)
    result = []
    start = 0
    for shape in shapes:
        size = 1
        for extent in shape:
            size *= extent
        result.append(mine[start : start + size].reshape(shape))
        start += size
    return result


def chain(own, decay, forward):
    members = lax.axis_size("tensor")
    if forward:
        hops = [(index, index + 1) for index in range(members - 1)]
    else:
        hops = [(index + 1, index) for index in range(members - 1)]
    held = None
    for _ in range(members - 1):
        value = own if held is None else own + decay * held.astype(F32)
        held = lax.ppermute(value.astype(BF), "tensor", hops)
    return held


def marks(bounds, rows, chunks):
    place = lax.axis_index("tensor")
    local = jnp.arange(rows, dtype=jnp.int32)[None, :]
    position = local + place * rows
    first = bounds[:, 0, 0:1]
    used = bounds[:, 0, 1:2]

    def segment_at(where):
        value = (where >= first).astype(jnp.int32) + (where >= used).astype(jnp.int32)
        return jnp.where(where < 0, -1, value)

    segment = segment_at(position)
    start = position - local % CHUNK
    columns = [segment == segment_at(position - back) for back in range(1, TAPS)]
    columns.append(segment == segment_at(start - 1))
    columns.append(segment == segment_at(start + CHUNK - 1))
    columns.append(segment)
    columns.append(position < used)
    columns.append(segment == segment_at(position * 0 + place * rows - 1))
    lane = lax.broadcasted_iota(jnp.int32, (1, 1, LANES), 2)
    table = jnp.zeros(segment.shape + (LANES,), F32)
    for index, column in enumerate(columns):
        table = jnp.where(lane == index, column.astype(F32)[:, :, None], table)
    across = jnp.broadcast_to(
        segment.astype(F32).reshape(-1, 1, CHUNK), (segment.shape[0] * chunks, 8, CHUNK)
    )
    return table.reshape(-1, LANES), across


def local(
    stream,
    bounds,
    prescale,
    expansion,
    timestep,
    selection,
    kernels,
    biases,
    stencil,
    baseline,
    offset,
    decays,
    passthrough,
    rescale,
    readout,
    cotangent,
):
    members = lax.axis_size("tensor")
    place = lax.axis_index("tensor")
    micro, rows = stream.shape[:2]
    chunks = rows // CHUNK
    assert rows * members == SLOT and bounds.shape[1] == 1
    weights = (prescale, expansion, timestep, selection, kernels, biases, stencil, baseline, offset, decays, passthrough, rescale, readout)
    got = gather_weights(weights)
    prescale_full = got[0].reshape(WIDTH).astype(F32)
    expand = join(got[1], 0, 2)
    time_full = join(got[2], 0, 1)
    select = got[3].reshape(WIDTH, 2 * STATE)
    kernel_full = join(got[4], 1, 0).reshape(INNER, TAPS)
    bias_full = join(got[5], 1, 0).reshape(INNER)
    stencil_full = got[6].reshape(2 * STATE, TAPS)
    baseline_full = got[7].reshape(2 * STATE)
    offset_full, decays_full, pass_full = (item[0].reshape(HEADS).astype(F32) for item in got[8:11])
    rescale_full = join(got[11], 1, 0).reshape(1, INNER).astype(F32)
    readout_full = join(got[12], 1, 0)

    head = lax.broadcasted_iota(jnp.int32, (LANES, INNER), 0)
    channel = lax.broadcasted_iota(jnp.int32, (LANES, INNER), 1) // HEAD_DIM
    spread = ((head < 2 * HEADS) & (head % HEADS == channel)).astype(BF)
    gather = ((head < HEADS) & (head == channel)).astype(BF).T
    pass_wide = jnp.repeat(pass_full, HEAD_DIM)
    taps = jnp.concatenate([kernel_full, stencil_full], axis=0).astype(F32).T
    shifts = jnp.concatenate([bias_full, baseline_full]).astype(F32)[None]
    last = jnp.concatenate([pass_wide, jnp.zeros((2 * STATE,), F32)])[None]
    taps = jnp.concatenate([taps, shifts, last, jnp.zeros((2, CHANNELS), F32)], axis=0)
    heads = jnp.pad(jnp.stack([offset_full, -jnp.exp(decays_full)]), ((0, 6), (0, LANES - HEADS)))
    cols, segrow = marks(bounds, rows, chunks)

    flat = stream.reshape(micro * rows, WIDTH)

    def low_norm(values):
        values = values.astype(F32)
        return (values * lax.rsqrt(jnp.mean(values * values, axis=-1, keepdims=True) + EPS) * prescale_full).astype(BF)

    hops = [(index, index + 1) for index in range(members - 1)]
    edge = lax.ppermute(stream[:, rows - 8 :, :], "tensor", hops).reshape(micro * 8, WIDTH)
    lowered = low_norm(flat)
    lowered_edge = low_norm(edge)
    signal_weight = jnp.concatenate([expand[:, 1, :], select], axis=1)
    gate_weight = expand[:, 0, :]
    time_weight = jnp.pad(time_full, ((0, 0), (0, LANES - HEADS)))
    signal = nn(lowered, signal_weight).astype(BF)
    signal_edge = nn(lowered_edge, signal_weight).astype(BF)
    gate = nn(lowered, gate_weight).astype(BF)
    sraw = nn(lowered, time_weight)
    tails = jnp.concatenate(
        [
            signal_edge.reshape(micro, 1, 8, CHANNELS),
            signal.reshape(micro, chunks, CHUNK, CHANNELS)[:, : chunks - 1, CHUNK - 8 :, :],
        ],
        axis=1,
    ).reshape(micro * chunks, 8, CHANNELS)
    core, convolved, maps, reach, states, decay = run_forward(
        signal, tails, sraw, cols, segrow, taps, heads, spread, chunks
    )
    total_decay = decay[:, chunks - 1, 0:1, :]
    enter = chain(states[:, chunks - 1].astype(F32), total_decay, True)

    reader = maps[:, STATE:]
    high = reach.astype(BF)
    reach_x = nn(high, gather.T) + nn((reach - high.astype(F32)).astype(BF), gather.T)
    brought = jnp.einsum(
        "min,mnk->mik", reader.reshape(micro, rows, STATE), enter, preferred_element_type=F32
    ).reshape(micro * rows, INNER)
    core = core + brought * reach_x
    conv_f = convolved.astype(F32)
    output = core + pass_wide * conv_f
    gate_f = gate.astype(F32)
    open_gate = jax.nn.sigmoid(gate_f)
    silu = gate_f * open_gate
    gated = output * silu
    inverse = lax.rsqrt(jnp.mean(gated * gated, axis=1, keepdims=True) + EPS)
    lifted = (gated * inverse * rescale_full).astype(BF)
    live = cols[:, 6:7]
    mixer = nn(lifted, readout_full)
    result = (flat.astype(F32) + live * mixer).astype(BF)
    cot = cotangent.reshape(micro * rows, WIDTH)
    back_mixer = jnp.where(live > 0, cot, jnp.zeros_like(cot))
    readout_term = tn(lifted, back_mixer)
    back_lifted = nt(back_mixer, readout_full)
    rescale_term = jnp.sum(back_lifted * gated * inverse, axis=0)
    weighted = back_lifted * rescale_full
    dots = jnp.sum(weighted * gated, axis=1, keepdims=True)
    back_gated = inverse * weighted - gated * (inverse * inverse * inverse) * (dots / INNER)
    out = (back_gated * silu).astype(BF)
    back_gate = (back_gated * output * open_gate * (1.0 + gate_f * (1.0 - open_gate))).astype(BF)
    out_f = out.astype(F32)
    pass_term = jnp.sum(jnp.sum(out_f * conv_f, axis=0).reshape(HEADS, HEAD_DIM), axis=1)
    row_sums = jnp.sum((out_f * core).reshape(micro * rows, HEADS, HEAD_DIM), axis=2)
    row_sums = jnp.pad(row_sums, ((0, 0), (0, LANES - HEADS)))
    back_enter = jnp.einsum(
        "min,mik->mnk",
        reader.reshape(micro, rows, STATE),
        (out_f * reach_x).astype(BF).reshape(micro, rows, INNER),
        preferred_element_type=F32,
    )
    back = chain(back_enter, total_decay, False)

    grad_signal, back_raw, halo, acc, head_acc = run_backward(
        signal, tails, sraw, cols, segrow, taps, heads, spread, gather, out, row_sums, states, decay, enter, back, chunks
    )
    returned = lax.ppermute(halo, "tensor", [(index + 1, index) for index in range(members - 1)])
    grad_signal = grad_signal.reshape(micro, rows, CHANNELS)
    fixed = (grad_signal[:, rows - 8 :].astype(F32) + returned.astype(F32)).astype(BF)
    grad_signal = lax.dynamic_update_slice_in_dim(grad_signal, fixed, rows - 8, 1).reshape(micro * rows, CHANNELS)

    gate_term = tn(lowered, back_gate)
    signal_term = tn(lowered, grad_signal)
    time_term = tn(lowered, back_raw)[:, :HEADS]
    back_lowered = nt(back_gate, gate_weight) + nt(grad_signal, signal_weight) + nt(back_raw, time_weight)
    values = flat.astype(F32)
    scale = lax.rsqrt(jnp.mean(values * values, axis=-1, keepdims=True) + EPS)
    prescale_term = jnp.sum(back_lowered * values * scale, axis=0)
    held = back_lowered * prescale_full
    grad_stream = held * scale - values * (scale * scale * scale) * jnp.mean(held * values, axis=-1, keepdims=True)
    grad_stream = (cot.astype(F32) + grad_stream).astype(BF)

    sums = jnp.sum(acc.reshape(5, 8, CHANNELS), axis=1)
    tap_terms = jnp.stack([sums[4], sums[3], sums[2], sums[1]], axis=1)
    head_sums = jnp.sum(head_acc.reshape(2, 8, LANES), axis=1)[:, :HEADS]
    grads = (
        prescale_term[:, None],
        jnp.stack([gate_term, signal_term[:, :INNER]], axis=1),
        time_term,
        signal_term[:, INNER:],
        tap_terms[:INNER].reshape(HEADS, HEAD_DIM * TAPS),
        sums[0, :INNER].reshape(HEADS, HEAD_DIM),
        tap_terms[INNER:],
        sums[0, INNER:][:, None],
        rescale_term.reshape(HEADS, HEAD_DIM),
        readout_term,
    )
    both = ((0, 0), (0, 2), (0, 1), (0, 0), (1, 0), (1, 0), (0, 0), (0, 0), (1, 0), (1, 0))
    shapes = [item.shape for item in (prescale, expansion, timestep, selection, kernels, biases, stencil, baseline, rescale, readout)]
    done = reduce_shards(grads, both, shapes)
    scalars = lax.psum(jnp.stack([head_sums[0], head_sums[1], pass_term]), ("dp", "tensor"))
    scalars = lax.dynamic_slice_in_dim(scalars, place * offset.shape[0], offset.shape[0], axis=1)
    return (
        result.reshape(stream.shape),
        grad_stream.reshape(stream.shape),
        done[0],
        done[1],
        done[2],
        done[3],
        done[4],
        done[5],
        done[6],
        done[7],
        scalars[0],
        scalars[1],
        scalars[2],
        done[8],
        done[9],
    )


def solution(mesh):
    everything = ("dp", "tensor")
    rows = P(None, everything, None)
    weights = (
        P(everything),
        P("dp", None, "tensor"),
        P("dp", "tensor"),
        P(everything, None),
        P("tensor", "dp"),
        P("tensor", "dp"),
        P(everything, None),
        P(everything),
        P("tensor"),
        P("tensor"),
        P("tensor"),
        P("tensor", "dp"),
        P("tensor", "dp"),
    )
    return jax.shard_map(
        local,
        mesh=mesh,
        in_specs=(rows, P(None, "dp", None)) + weights + (rows,),
        out_specs=(rows, rows) + weights,
        check_vma=False,
    )
```

time: 1640 us -> 1020 us (0.62)
  blocking collectives: 369 us -> 44.6 us
  matrix products: 355 us -> 137 us
  other arithmetic: 296 us -> 83.6 us
  Pallas kernels: 0 us -> 125 us
  local copies, waits for them, and re-layouts: 206 us -> 314 us
  waiting for transfers between devices: 386 us -> 278 us
    reduce_scatter x14 -> x0, waiting for transfers between devices: 319 us -> none  [the longest x4 103 us: local(): lax.psum_scatter(back_lowered.astype(jnp.bfloat16), 'tensor', scatter_dim...]
    all_gather x6 -> x0, blocking collectives: 207 us -> none  [the longest x1 67 us: local(): lax.all_gather(selection, ('dp', 'tensor'), axis=0, tiled=True)]
    dot_general x104 -> x17, matrix products: 333 us -> 137 us  [the longest x7 62.2 us: nn(): lax.dot_general(a, b, (((1,), (0,)), ((), ())), preferred_element_type=F32)]
    unnamed x30 -> x4, waiting for transfers between devices: 67.2 us -> 261 us
    pallas_call x0 -> x2, Pallas kernels: none -> 125 us  [the longest x1 88 us: run_backward(): pl.pallas_call(scan_backward, grid=(micro, chunks), in_specs=[flat(CHANNE...]
    unnamed x3 -> x0, blocking collectives: 114 us -> none
    another operation x21 -> x3, other arithmetic: 65.7 us -> 0.66 us  [the longest x1 0.6 us: local(): jnp.stack([offset_full, -jnp.exp(decays_full)])]
    reduce_sum x23 -> x7, other arithmetic: 94.6 us -> 30.7 us  [the longest x1 22.2 us: local(): jnp.sum(out_f * conv_f, axis=0).reshape(HEADS, HEAD_DIM)]
  transfers between devices with their start and end apart: 27 -> 6, of which waited for: 10 -> 3; matrix products, arithmetic and copies ran while one was open for 29% -> 15% of each run, Pallas kernels for 0% -> 0%
where the time goes in v1:
time: 1020 us; the launch traced here: 1010 us
  local copies, waits for them, and re-layouts  314 us (31%)
  waiting for transfers between devices  278 us (27%)
  matrix products  137 us (13%)
  Pallas kernels  125 us (12%)
  other arithmetic  83.6 us (8%)
  blocking collectives  44.6 us (4%)
  between operations  15.5 us (2%)
  starting transfers between devices  12.4 us (1%)
    unnamed x4, waiting for transfers between devices  261 us
    pallas_call x1, Pallas kernels, run_backward(): pl.pallas_call(scan_backward, grid=(micro, chunks), in_specs=[flat(CHANNE...  88 us
    unnamed x165, local copies, waits for them, and re-layouts  68.4 us
    dot_general x7, matrix products, nn(): lax.dot_general(a, b, (((1,), (0,)), ((), ())), preferred_element_type=F32)  62.2 us
    psum x1, blocking collectives, local(): lax.psum(jnp.stack([head_sums[0], head_sums[1], pass_term]), ('dp', 'tens...  44.6 us
    pallas_call x1, Pallas kernels, run_forward(): pl.pallas_call(scan_forward, grid=(micro, chunks), in_specs=[flat(CHANNEL...  36.9 us
    dot_general x4, matrix products, tn(): lax.dot_general(a, b, (((0,), (0,)), ((), ())), preferred_element_type=F32)  31.4 us
    reshape x5, local copies, waits for them, and re-layouts, gather_weights(): everyone[:, :, start:start + shard.size]  31.2 us
  transfers between devices with their start and end apart: 6, of which 3 were waited for; matrix products, arithmetic and copies ran while one was open for 15% of the time, Pallas kernels for 0%

profile of v1, /device:TPU:0, one launch (start us, length us, event | category | flops | bytes accessed | tf_op | source)
XLA Modules:
  0.0 1009.8 jit_solution(17388117571560222507)
XLA Ops:
  14.6 6.2 concatenate.37
  24.3 4.6 dynamic-update-slice
  29.1 4.9 collective-permute-start
  51.5 150.7 %all-reduce.9.cloned.1.call-done = bf16[3766400]{0:T(1024)(128)(2,1)} async-done(((bf16[3766400]{0:T(1024)(128)(2,1)}), bf16[3766400]{0:T(1024)(128)(2,1)}) %all-reduce.9.cloned.1.call-update) | async-done | bytes 7532816
  202.2 12.7 %reshape.1346 = bf16[16,2,117700]{2,1,0:T(2,128)(2,1)} reshape(bf16[3766400]{0:T(1024)(128)(2,1)} %all-reduce.9.cloned.1.call-done) | data formatting | bytes 15065600 | tf_op jit(solution)/shard_map/reshape | solution.py:443
  214.8 5.7 slice.255
  223.4 10.0 slice.240
  243.1 4.4 copy.257
  247.5 8.6 reshape.1359
  256.1 9.4 copy.258
  271.4 11.7 %reshape.1347 = bf16[16,2,48,2,768]{4,3,2,1,0:T(2,128)(2,1)} reshape(bf16[16,2,73728]{2,1,0:T(2,128)(2,1)} %slice.240) | data formatting | bytes 9437184 | tf_op jit(solution)/shard_map/reshape | solution.py:447
  283.1 9.5 copy.307
  292.6 11.4 %reshape.1348 = bf16[768,2,1536]{2,0,1:T(8,128)(2,1)} reshape(bf16[16,48,2,2,768]{4,3,1,0,2:T(2,128)(2,1)} %bitcast.242) | data formatting | bytes 9437184 | tf_op jit(solution)/shard_map/reshape | solution.py:465
  306.7 6.1 convolution_convert_fusion.1.x_ref
  320.5 3.8 fusion.46.sraw_ref
  340.9 36.9 %scan_forward.1 = (f32[2048,1536]{1,0:T(8,128)}, bf16[2048,1536]{1,0:T(8,128)(2,1)}, bf16[2048,256]{1,0:T(8,128)(2,1)}, f32[2048,128]{1,0:T(8,128)}, bf16[4,4,12...) custom-call(bf16[2048,1792]{1,0:T(8,128)(2,1)} %copy-done.5, bf16[16,8,1792]{2,1,0:T(8,128)(2,1)} %bitcast.252, ...), custom_call_target="tpu_custom_call" | custom-call | tf_op jit(solution)/shard_map/scan_forward/pallas_call | solution.py:357
  382.4 4.5 collective-permute-start.1
  389.9 5.2 copy.263
  396.9 6.4 convolution_add_fusion
  403.4 16.4 %collective-permute-done.1.enter_ref = bf16[4,128,1536]{2,1,0:T(8,128)(2,1)} collective-permute-done((bf16[4,128,1536]{2,1,0:T(8,128)(2,1)}, bf16[4,128,1536]{2,1,0:T(8,128)(2,1)}, u32[]{:S(2)}, u32[]{:S(2)}) %collective-permute-start.1) | collective-permute-done | bytes 1572896 | tf_op jit(solution)/shard_map/ppermute | solution.py:511
  419.8 7.7 fusion.85
  427.5 31.5 %multiply_reduce_fusion.2 = (f32[2048]{0:T(1024)S(1)}, f32[2048,1536]{1,0:T(8,128)}, f32[2048,1536]{1,0:T(8,128)}, bf16[2048,1536]{1,0:T(8,128)(2,1)}) fusion(bf16[2048,1536]{1,0:T(8,128)(2,1)} %get-tuple-element.30, f32[1536]{0:T(1024)S(1)} %copy-done.31, f32[2048,1536]{1,0:T(8,128)} %get-tuple-element.26, f32[2048,1536]{1,0:T(8,128)} %convolution_add_fusion, ...), kind=kOutput, calls=%fused_computation.23 | convolution fusion | flops 4875876352 | bytes 81016832 | tf_op jit(solution)/shard_map/dot_general | solution.py:28
  459.0 12.8 %multiply_reduce_fusion = (bf16[1536]{0:T(1024)(128)(2,1)S(1)}, f32[2048]{0:T(1024)S(1)}, f32[2048,1536]{1,0:T(8,128)}) fusion(f32[2048,1536]{1,0:T(8,128)} %get-tuple-element.136, f32[2048]{0:T(1024)S(1)} %get-tuple-element.159, f32[1536]{0:T(1024)S(1)} %reshape.1390, bf16[2048,768]{1,0:T(8,128)(2,1)} %bitcast.254, bf16[1536,768]{0,1:T(8,128)(2,1)} %bitcast.258), kind=kOutput, calls=%fused_computation.18 | convolution fusion | flops 4850708992 | bytes 30696448 | tf_op jit(solution)/shard_map/dot_general | solution.py:32
  471.8 22.2 %fusion.8 = (f32[1536]{0:T(1024)}, bf16[2048,1536]{1,0:T(8,128)(2,1)S(1)}, bf16[2048,1536]{1,0:T(8,128)(2,1)}) fusion(bf16[2048,1536]{1,0:T(8,128)(2,1)} %get-tuple-element.30, bf16[2048,1536]{1,0:T(8,128)(2,1)} %get-tuple-element.167, f32[2048]{0:T(1024)S(1)} %broadcast_multiply_fusion.1, f32[2048,1536]{1,0:T(8,128)} %get-tuple-element.136, ...), kind=kLoop, calls=%fused_computation.15 | loop fusion | flops 78641664 | bytes 62957568 | tf_op jit(solution)/shard_map/reduce_sum | solution.py:652
  494.0 15.1 %fusion.7 = (bf16[2048,1536]{1,0:T(8,128)(2,1)}, f32[2048,1536]{1,0:T(8,128)}) fusion(f32[2048,1536]{1,0:T(8,128)S(1)} %bitcast.234, bf16[2048,1536]{1,0:T(8,128)(2,1)S(1)} %get-tuple-element.134.out_ref, f32[2048,1536]{1,0:T(8,128)} %get-tuple-element.137), kind=kLoop, calls=%fused_computation.14 | loop fusion | flops 12582912 | bytes 50331648 | tf_op jit(solution)/shard_map/convert_element_type | solution.py:658
  509.1 5.1 convolution_convert_fusion.3
  515.9 10.5 %convolution_convert_fusion.2 = bf16[1536,768]{1,0:T(8,128)(2,1)} fusion(bf16[2048,768]{1,0:T(8,128)(2,1)S(1)} %copy-done.10, f32[2048,1536]{1,0:T(8,128)} %get-tuple-element.136, f32[1536]{0:T(1024)S(1)} %reshape.1390, f32[2048]{0:T(1024)S(1)} %get-tuple-element.159), kind=kOutput, calls=%fused_computation.52 | convolution fusion | flops 4842455040 | bytes 18102272 | tf_op jit(solution)/shard_map/dot_general | solution.py:36
  526.4 7.0 fusion.25
  533.4 12.7 %copy.260 = f32[2048,1536]{0,1:T(8,128)} copy(f32[2048,1536]{1,0:T(8,128)} %get-tuple-element.147) | data formatting | bytes 25165824 | tf_op jit(solution)/shard_map/mul | solution.py:653
  546.1 6.4 reduce_sum.116
  553.9 8.7 copy.289
  568.6 9.4 copy.276
  578.0 14.7 %reshape.1377 = bf16[32,36864]{1,0:T(8,128)(2,1)} reshape(bf16[16,2,768,48]{3,2,1,0:T(8,128)(2,1)} %copy.276) | data formatting | bytes 4718592 | tf_op jit(solution)/shard_map/reshape | solution.py:488
  592.7 9.3 convert_bitcast_fusion
  601.9 88.0 %scan_backward.1 = (bf16[2048,1792]{1,0:T(8,128)(2,1)}, bf16[2048,128]{1,0:T(8,128)(2,1)}, bf16[4,8,1792]{2,1,0:T(8,128)(2,1)}, f32[40,1792]{1,0:T(8,128)}, f32[16,128]{1,0:T(8,128)}) custom-call(bf16[2048,1792]{1,0:T(8,128)(2,1)} %copy-done.5, bf16[16,8,1792]{2,1,0:T(8,128)(2,1)} %bitcast.253, f32[2048,128]{1,0:T(8,128)} %fusion.46.sraw_ref, ...), custom_call_target="tpu_custom_call" | custom-call | tf_op jit(solution)/shard_map/scan_backward/pallas_call | solution.py:397
  708.8 9.9 bitcast_convert_fusion
  721.4 6.1 fusion.26
  727.6 5.0 fusion.23
  733.3 6.1 stack.23
  744.3 9.4 copy.267
  753.7 6.8 reshape.1369
  762.9 27.5 %dynamic-update-slice.2 = bf16[32,117664]{1,0:T(8,128)(2,1)} dynamic-update-slice(bf16[32,117664]{1,0:T(8,128)(2,1)} %dynamic-update-slice.1, bf16[32,73728]{1,0:T(8,128)(2,1)} %reshape.1369, s32[]{} %constant.158, s32[]{} %constant.159) | dynamic-update-slice | bytes 9437188
  792.1 3.9 dynamic-update-slice.4
  803.7 14.3 %dynamic-update-slice.10 = bf16[32,117664]{1,0:T(8,128)(2,1)} dynamic-update-slice(bf16[32,117664]{1,0:T(8,128)(2,1)} %dynamic-update-slice.9, bf16[32,36864]{1,0:T(8,128)(2,1)} %reshape.1377, s32[]{} %constant.158, s32[]{} %constant.167) | dynamic-update-slice | bytes 4718596 | tf_op jit(solution)/shard_map/concatenate | solution.py:487
  820.1 10.0 fusion.16
  830.1 44.6 %psum.7 = f32[3,24]{1,0:T(4,128)S(1)} all-reduce(f32[3,24]{1,0:T(4,128)S(1)} %pad_maximum_fusion.5), channel_id=1, replica_groups=mesh['dp'=16,'tensor'=2] {'dp','tensor'}, use_global_device_ids=true, to_apply=%region_13.14 | all-reduce | flops 72 | bytes 576 | tf_op jit(solution)/shard_map/psum | solution.py:700
  875.3 5.8 fusion.20
  881.2 110.7 %all-reduce.11.cloned.1.call-done = bf16[32,117664]{1,0:T(8,128)(2,1)} async-done(((bf16[32,117664]{1,0:T(8,128)(2,1)}), bf16[32,117664]{1,0:T(8,128)(2,1)}) %all-reduce.11.cloned.1.call-update) | async-done | bytes 7530512
  (352 shorter events, 144.0 us)
Async XLA Ops:
  7.2 195.0 %all-reduce.9.cloned.1.call-start = ((), (), s32[]{:S(2)}) async-start(), calls=%async_computation | async-start | bytes 15069184
  20.8 8.3 copy-start
  20.8 13.5 %copy-start.50 = (s32[4,1,2]{0,2,1:T(2,128)S(1)}, s32[4,1,2]{0,2,1:T(2,128)}, u32[]{:S(2)}) copy-start(s32[4,1,2]{0,2,1:T(2,128)} %param.17) | copy-start | bytes 100
  29.0 962.9 %all-reduce.11.cloned.1.call-start = ((), (), s32[]{:S(2)}) async-start(), calls=%async_computation.1 | async-start | bytes 15073280
  29.1 21.7 %collective-permute-start = (bf16[4,8,768]{2,1,0:T(8,128)(2,1)S(1)}, bf16[4,8,768]{2,1,0:T(8,128)(2,1)S(1)}, u32[]{:S(2)}, u32[]{:S(2)}) collective-permute-start(bf16[4,8,768]{2,1,0:T(8,128)(2,1)S(1)} %slice.192), channel_id=1, source_target_pairs={{0,1},{2,3},{4,5},{6,7},{8,9},{10,11},{12,13},{14,15},{16,17},{18,... | collective-permute-start | bytes 147464 | tf_op jit(solution)/shard_map/ppermute | solution.py:600
  38.8 7.8 copy-start.6
  38.9 10.1 copy-start.48
  38.9 10.0 copy-start.33
  50.8 164.1 %copy-start.35 = (bf16[4,8,768]{2,1,0:T(8,128)(2,1)}, bf16[4,8,768]{2,1,0:T(8,128)(2,1)S(1)}, u32[]{:S(2)}) copy-start(bf16[4,8,768]{2,1,0:T(8,128)(2,1)S(1)} %collective-permute-done) | copy-start | bytes 147460
  292.6 13.3 %copy-start.23 = (f32[1,4,4,128]{3,1,2,0:T(4,128)S(1)}, f32[1,4,4,128]{3,1,2,0:T(4,128)}, u32[]{:S(2)}) copy-start(f32[1,4,4,128]{3,1,2,0:T(4,128)} %copy.300) | copy-start | bytes 24580
  292.6 13.3 %copy-start.27 = (f32[768]{0:T(1024)S(1)}, f32[768]{0:T(1024)}, u32[]{:S(2)}) copy-start(f32[768]{0:T(1024)} %reshape.1386) | copy-start | bytes 9220
  305.9 6.9 copy-start.14
  306.7 9.8 copy-start.25
  319.4 7.6 copy-start.43
  319.4 8.3 copy-start.32
  340.9 46.0 %copy-start.28 = (f32[768]{0:T(1024)S(1)}, f32[768]{0:T(1024)}, u32[]{:S(2)}) copy-start(f32[768]{0:T(1024)} %reshape.1386) | copy-start | bytes 9220
  340.9 46.0 %copy-start.40 = (f32[4,512]{1,0:T(4,128)S(1)}, f32[4,512]{1,0:T(4,128)}, u32[]{:S(2)}) copy-start(f32[4,512]{1,0:T(4,128)} %get-tuple-element.161) | copy-start | bytes 24580
  377.8 11.6 %copy-start.44 = (bf16[16,2,48]{2,1,0:T(2,128)(2,1)S(1)}, bf16[16,2,48]{2,1,0:T(2,128)(2,1)}, u32[]{:S(2)}) copy-start(bf16[16,2,48]{2,1,0:T(2,128)(2,1)} %get-tuple-element.142) | copy-start | bytes 9220
  382.4 37.4 %collective-permute-start.1 = (bf16[4,128,1536]{2,1,0:T(8,128)(2,1)}, bf16[4,128,1536]{2,1,0:T(8,128)(2,1)}, u32[]{:S(2)}, u32[]{:S(2)}) collective-permute-start(bf16[4,128,1536]{2,1,0:T(8,128)(2,1)} %slice_bitcast_fusion.4), channel_id=1, source_target_pairs={{0,1},{2,3},{4,5},{6,7},{8,9},{10,11},{12,13},{14,15},{16,17},{18,... | collective-permute-start | bytes 4718600 | tf_op jit(solution)/shard_map/ppermute | solution.py:511
  386.9 8.1 copy-start.34
  386.9 8.1 copy-start.49
  389.8 126.0 %copy-start.36 = (f32[1536]{0:T(1024)}, f32[1536]{0:T(1024)S(1)}, u32[]{:S(2)}) copy-start(f32[1536]{0:T(1024)S(1)} %reshape.1390) | copy-start | bytes 18436
  396.9 22.9 %copy-start.9 = (bf16[2048,128]{1,0:T(8,128)(2,1)S(1)}, bf16[2048,128]{1,0:T(8,128)(2,1)}, u32[]{:S(2)}) copy-start(bf16[2048,128]{1,0:T(8,128)(2,1)} %slice.202) | copy-start | bytes 1572868
  419.8 7.7 copy-start.31
  459.0 56.8 %copy-start.38 = (f32[2048]{0:T(1024)}, f32[2048]{0:T(1024)S(1)}, u32[]{:S(2)}) copy-start(f32[2048]{0:T(1024)S(1)} %get-tuple-element.159) | copy-start | bytes 24580
  459.0 35.0 %slice-start = ((s8[12582912]{0:T(1024)(128)(4,1)}), s8[4194304]{0:T(1024)(128)(4,1)S(1)}, s32[]{:S(2)}) async-start(s8[12582912]{0:T(1024)(128)(4,1)} %bitcast.233), calls=%async_computation.2 | async-start | bytes 8388608
  459.0 35.0 %slice-start.1 = ((s8[12582912]{0:T(1024)(128)(4,1)}), s8[4194304]{0:T(1024)(128)(4,1)S(1)}, s32[]{:S(2)}) async-start(s8[12582912]{0:T(1024)(128)(4,1)} %bitcast.233), calls=%async_computation.3 | async-start | bytes 8388608
  471.8 22.2 %slice-start.2 = ((s8[12582912]{0:T(1024)(128)(4,1)}), s8[4194304]{0:T(1024)(128)(4,1)S(1)}, s32[]{:S(2)}) async-start(s8[12582912]{0:T(1024)(128)(4,1)} %bitcast.233), calls=%async_computation.4 | async-start | bytes 8388608
  494.0 15.1 %copy-start.2 = (bf16[2048,1536]{1,0:T(8,128)(2,1)}, bf16[2048,1536]{1,0:T(8,128)(2,1)S(1)}, u32[]{:S(2)}) copy-start(bf16[2048,1536]{1,0:T(8,128)(2,1)S(1)} %get-tuple-element.134.out_ref) | copy-start | bytes 18874372
  509.1 17.2 %slice-start.3 = ((s8[6291456]{0:T(1024)(128)(4,1)}), s8[4194304]{0:T(1024)(128)(4,1)S(1)}, s32[]{:S(2)}) async-start(s8[6291456]{0:T(1024)(128)(4,1)} %bitcast.240), calls=%async_computation.5 | async-start | bytes 8388608
  509.1 17.2 %slice-start.5 = ((s8[4718592]{0:T(1024)(128)(4,1)}), s8[4194304]{0:T(1024)(128)(4,1)S(1)}, s32[]{:S(2)}) async-start(s8[4718592]{0:T(1024)(128)(4,1)} %bitcast.243), calls=%async_computation.7 | async-start | bytes 8388608
  514.3 12.1 %slice-start.4 = ((s8[6291456]{0:T(1024)(128)(4,1)}), s8[2097152]{0:T(1024)(128)(4,1)S(1)}, s32[]{:S(2)}) async-start(s8[6291456]{0:T(1024)(128)(4,1)} %bitcast.240), calls=%async_computation.6 | async-start | bytes 4194304
  514.3 12.1 %slice-start.6 = ((s8[4718592]{0:T(1024)(128)(4,1)}), s8[524288]{0:T(1024)(128)(4,1)S(1)}, s32[]{:S(2)}) async-start(s8[4718592]{0:T(1024)(128)(4,1)} %bitcast.243), calls=%async_computation.8 | async-start | bytes 1048576
  514.3 87.7 %collective-permute-start.2 = (bf16[4,128,1536]{2,1,0:T(8,128)(2,1)}, bf16[4,128,1536]{2,1,0:T(8,128)(2,1)}, u32[]{:S(2)}, u32[]{:S(2)}) collective-permute-start(bf16[4,128,1536]{2,1,0:T(8,128)(2,1)} %convolution_convert_fusion.3), channel_id=1, source_target_pairs={{1,0},{3,2},{5,4},{7,6},{9,8},{11,10},{13,12},{15,14},{17,16},{19,... | collective-permute-start | bytes 4718600 | tf_op jit(solution)/shard_map/ppermute | solution.py:511
  578.0 14.7 %copy-start.11 = (bf16[768,2048]{1,0:T(8,128)(2,1)S(1)}, bf16[768,2048]{1,0:T(8,128)(2,1)}, u32[]{:S(2)}) copy-start(bf16[768,2048]{1,0:T(8,128)(2,1)} %copy.263) | copy-start | bytes 9437188
  601.9 91.1 %copy-start.4 = (bf16[2048,768]{1,0:T(8,128)(2,1)S(1)}, bf16[2048,768]{1,0:T(8,128)(2,1)}, u32[]{:S(2)}) copy-start(bf16[2048,768]{1,0:T(8,128)(2,1)} %copy-done.3) | copy-start | bytes 9437188
  689.9 18.9 %copy-start.12 = (bf16[4,512,768]{2,1,0:T(8,128)(2,1)S(1)}, bf16[4,512,768]{2,1,0:T(8,128)(2,1)}, u32[]{:S(2)}) copy-start(bf16[4,512,768]{2,1,0:T(8,128)(2,1)} %fusion.13) | copy-start | bytes 9437188
  691.8 15.4 %collective-permute-start.3 = (bf16[4,8,1792]{2,1,0:T(8,128)(2,1)}, bf16[4,8,1792]{2,1,0:T(8,128)(2,1)}, u32[]{:S(2)}, u32[]{:S(2)}) collective-permute-start(bf16[4,8,1792]{2,1,0:T(8,128)(2,1)} %get-tuple-element.33), channel_id=1, source_target_pairs={{1,0},{3,2},{5,4},{7,6},{9,8},{11,10},{13,12},{15,14},{17,16},{19,... | collective-permute-start | bytes 344072 | tf_op jit(solution)/shard_map/ppermute | solution.py:666
  708.8 12.6 %copy-start.15 = (bf16[768,1536]{1,0:T(8,128)(2,1)S(1)}, bf16[768,1536]{1,0:T(8,128)(2,1)}, u32[]{:S(2)}) copy-start(bf16[768,1536]{1,0:T(8,128)(2,1)} %copy-done.14) | copy-start | bytes 7077892
  708.8 12.6 %copy-start.20 = (bf16[768,256]{1,0:T(8,128)(2,1)S(1)}, bf16[768,256]{1,0:T(8,128)(2,1)}, u32[]{:S(2)}) copy-start(bf16[768,256]{1,0:T(8,128)(2,1)} %reshape_reshape.19) | copy-start | bytes 1179652
  708.8 12.6 %copy-start.51 = (bf16[4,512,1792]{2,1,0:T(8,128)(2,1)S(1)}, bf16[4,512,1792]{2,1,0:T(8,128)(2,1)}, u32[]{:S(2)}) copy-start(bf16[4,512,1792]{2,1,0:T(8,128)(2,1)} %fusion.48) | copy-start | bytes 22020100
  718.8 8.8 slice-start.7
  761.5 30.6 %copy-start.17 = (bf16[32,6144]{1,0:T(8,128)(2,1)S(1)}, bf16[32,6144]{1,0:T(8,128)(2,1)}, u32[]{:S(2)}) copy-start(bf16[32,6144]{1,0:T(8,128)(2,1)} %reshape_reshape.22) | copy-start | bytes 1179652
  803.7 16.2 %copy-start.41 = (f32[1536]{0:T(1024)S(1)}, f32[1536]{0:T(1024)}, u32[]{:S(2)}) copy-start(f32[1536]{0:T(1024)} %get-tuple-element.133) | copy-start | bytes 18436
  803.7 16.4 %copy-start.37 = (f32[1536]{0:T(1024)S(1)}, f32[1536]{0:T(1024)}, u32[]{:S(2)}) copy-start(f32[1536]{0:T(1024)} %copy-done.36) | copy-start | bytes 18436
  803.7 16.4 %copy-start.39 = (f32[2048]{0:T(1024)S(1)}, f32[2048]{0:T(1024)}, u32[]{:S(2)}) copy-start(f32[2048]{0:T(1024)} %copy-done.38) | copy-start | bytes 24580
  820.1 10.0 copy-start.47
  820.1 55.3 %copy-start.42 = (f32[2048]{0:T(1024)S(1)}, f32[2048]{0:T(1024)}, u32[]{:S(2)}) copy-start(f32[2048]{0:T(1024)} %get-tuple-element.130) | copy-start | bytes 24580
  (21 other events, 101.8 us)
Sparse Core Ops, SparseCore 0:
  29.1 173.0 all-reduce.8
  818.1 173.8 all-reduce.10

commit v2 on v1

--- a/solution.py
+++ b/solution.py
@@ -437,6 +437,408 @@
     )(x, tails, sraw, cols, segrow, taps, heads, spread, gather, out, row_sums, states, decay, enter, back)
 
 
+def fold(value):
+    rows, lanes = value.shape
+    return jnp.sum(value.reshape(rows // 8, 8, lanes), axis=0)
+
+
+def mixer_kernel(
+    core_ref,
+    conv_ref,
+    gate_ref,
+    maps_ref,
+    reach_ref,
+    enter_ref,
+    cols_ref,
+    stream_ref,
+    cot_ref,
+    readout_ref,
+    taps_ref,
+    rescale_ref,
+    spread_ref,
+    gather_ref,
+    result_ref,
+    masked_ref,
+    lifted_ref,
+    out_ref,
+    back_gate_ref,
+    rows_ref,
+    back_enter_ref,
+    acc_ref,
+    core_s,
+    gated_s,
+    silu_s,
+    slope_s,
+    back_s,
+    reach_s,
+    enter_s,
+):
+    rows = core_ref.shape[0]
+
+    @pl.when((pl.program_id(0) == 0) & (pl.program_id(1) == 0))
+    def _():
+        acc_ref[...] = jnp.zeros_like(acc_ref)
+
+    @pl.when(pl.program_id(1) == 0)
+    def _():
+        enter_s[...] = jnp.zeros_like(enter_s)
+
+    reader = maps_ref[:, STATE:]
+    reach2 = doubled(reach_ref[...])
+    squares = jnp.zeros((rows, GROUP), F32)
+    for group in range(INNER // GROUP):
+        span = slice(group * GROUP, (group + 1) * GROUP)
+        reach_x = nn(reach2, spread_ref[:, span])
+        reach_s[:, span] = reach_x
+        core = core_ref[:, span] + nn(reader, enter_ref[0, :, span]) * reach_x
+        core_s[:, span] = core
+        output = core + taps_ref[5:6, span] * conv_ref[:, span].astype(F32)
+        gate = gate_ref[:, span].astype(F32)
+        opened = sigmoid(gate)
+        silu = gate * opened
+        gated = output * silu
+        gated_s[:, span] = gated
+        silu_s[:, span] = silu
+        slope_s[:, span] = output * opened * (1.0 + gate * (1.0 - opened))
+        squares = squares + gated * gated
+    inverse = lax.rsqrt(jnp.sum(squares, axis=1, keepdims=True) / INNER + EPS)
+    for group in range(INNER // GROUP):
+        span = slice(group * GROUP, (group + 1) * GROUP)
+        lifted_ref[:, span] = (gated_s[:, span] * inverse * rescale_ref[0:1, span]).astype(BF)
+    mixer = nt(lifted_ref[...], readout_ref[...])
+    live = cols_ref[:, 6:7]
+    result_ref[...] = (stream_ref[...].astype(F32) + live * mixer).astype(BF)
+    masked = jnp.where(live > 0, cot_ref[...].astype(F32), 0.0).astype(BF)
+    masked_ref[...] = masked
+    terms = jnp.zeros((rows, GROUP), F32)
+    for group in range(INNER // GROUP):
+        span = slice(group * GROUP, (group + 1) * GROUP)
+        back = nn(masked, readout_ref[:, span])
+        product = back * gated_s[:, span]
+        acc_ref[0:8, span] += fold(product * inverse)
+        terms = terms + product * rescale_ref[0:1, span]
+        back_s[:, span] = back * rescale_ref[0:1, span]
+    dots = jnp.sum(terms, axis=1, keepdims=True)
+    pull = inverse * inverse * inverse * (dots / INNER)
+    reader_t = jnp.transpose(reader.astype(F32)).astype(BF)
+    sums = jnp.zeros((rows, LANES), F32)
+    for group in range(INNER // GROUP):
+        span = slice(group * GROUP, (group + 1) * GROUP)
+        back_gated = inverse * back_s[:, span] - gated_s[:, span] * pull
+        out = (back_gated * silu_s[:, span]).astype(BF)
+        out_ref[:, span] = out
+        back_gate_ref[:, span] = (back_gated * slope_s[:, span]).astype(BF)
+        out_f = out.astype(F32)
+        acc_ref[8:16, span] += fold(out_f * conv_ref[:, span].astype(F32))
+        high, low = pieces(out_f * core_s[:, span])
+        sums = sums + nn(high, gather_ref[span, :]) + nn(low, gather_ref[span, :])
+        enter_s[:, span] += nn(reader_t, (out_f * reach_s[:, span]).astype(BF))
+    rows_ref[...] = sums
+    back_enter_ref[0] = enter_s[...].astype(BF)
+
+
+def run_mixer(core, convolved, gate, maps, reach, enter, cols, stream, cot, readout, taps, rescale, spread, gather, micro):
+    total = core.shape[0]
+    tile = min(256, total // micro)
+    steps = total // micro // tile
+    flat = lambda width: pl.BlockSpec((tile, width), lambda m, c: (m * steps + c, 0))
+    state = pl.BlockSpec((1, STATE, INNER), lambda m, c: (m, 0, 0))
+    wide_scratch = pltpu.VMEM((tile, INNER), F32)
+    return pl.pallas_call(
+        mixer_kernel,
+        grid=(micro, steps),
+        in_specs=[
+            flat(INNER),
+            flat(INNER),
+            flat(INNER),
+            flat(2 * STATE),
+            flat(LANES),
+            state,
+            flat(LANES),
+            flat(WIDTH),
+            flat(WIDTH),
+            constant((WIDTH, INNER)),
+            constant((8, CHANNELS)),
+            constant((8, INNER)),
+            constant((LANES, INNER)),
+            constant((INNER, LANES)),
+        ],
+        out_specs=[
+            flat(WIDTH),
+            flat(WIDTH),
+            flat(INNER),
+            flat(INNER),
+            flat(INNER),
+            flat(LANES),
+            state,
+            constant((16, INNER)),
+        ],
+        out_shape=[
+            jax.ShapeDtypeStruct((total, WIDTH), BF),
+            jax.ShapeDtypeStruct((total, WIDTH), BF),
+            jax.ShapeDtypeStruct((total, INNER), BF),
+            jax.ShapeDtypeStruct((total, INNER), BF),
+            jax.ShapeDtypeStruct((total, INNER), BF),
+            jax.ShapeDtypeStruct((total, LANES), F32),
+            jax.ShapeDtypeStruct((micro, STATE, INNER), BF),
+            jax.ShapeDtypeStruct((16, INNER), F32),
+        ],
+        scratch_shapes=[wide_scratch] * 6 + [pltpu.VMEM((STATE, INNER), F32)],
+        compiler_params=pltpu.CompilerParams(vmem_limit_bytes=VMEM_LIMIT),
+        name="gated_mixer",
+    )(core, convolved, gate, maps, reach, enter, cols, stream, cot, readout, taps, rescale, spread, gather)
+
+MESH = pl.DeviceIdType.MESH
+
+
+def places():
+    dp = lax.axis_index("dp")
+    tensor = lax.axis_index("tensor")
+    return {"Z": dp // 8, "z": (dp // 4) % 2, "x": (dp // 2) % 2, "c": dp % 2, "t": tensor}
+
+
+def partner(at, axis):
+    to = dict(at)
+    to[axis] = 1 - at[axis]
+    return (to["Z"] * 8 + to["z"] * 4 + to["x"] * 2 + to["c"], to["t"])
+
+
+def greet(at):
+    barrier = pltpu.get_barrier_semaphore()
+    for axis in ("Z", "z", "x", "c", "t"):
+        pl.semaphore_signal(barrier, inc=1, device_id=partner(at, axis), device_id_type=MESH)
+    pl.semaphore_wait(barrier, 5)
+
+
+GATHER_ORDERS = (("Z", "z", "x", "t", "c"), ("Z", "z", "t", "x", "c"))
+SCATTER_ORDERS = (("c", "t", "x", "z", "Z"), ("c", "x", "t", "z", "Z"))
+AXES = ("Z", "z", "x", "t")
+HALF = INNER // 4
+SMALL = ("small", 0)
+SELECT = ("select", 0)
+CHAINS = (SMALL, (0, 0), (0, 1), SELECT, (1, 0), (1, 1), (2, 0), (2, 1))
+DELAYS = (0, 0, 0, 0, 1, 1, 2, 2)
+
+
+def half_lanes(tensor, half):
+    return pl.ds(pl.multiple_of(tensor * (INNER // 2) + half * HALF, LANES), HALF)
+
+
+def order_of(chain, orders):
+    return orders[1] if chain == SMALL else orders[chain[1]]
+
+
+def gather_kernel(main_ref, select_ref, small_ref, whole_ref, selects_ref, smalls_ref, send, recv, own):
+    at = places()
+    greet(at)
+
+    def source(chain):
+        piece, half = chain
+        if chain == SELECT:
+            return select_ref
+        if chain == SMALL:
+            return small_ref
+        return main_ref.at[piece, :, half * HALF : (half + 1) * HALF]
+
+    def views(chain, done):
+        piece, half = chain
+        index = tuple(slice(None) if axis in done else at[axis] for axis in ("Z", "z", "x", "c"))
+        tensors = range(2) if "t" in done else [at["t"]]
+        if chain in (SELECT, SMALL):
+            whole = selects_ref if chain == SELECT else smalls_ref
+            return [whole.at[index + (slice(None) if "t" in done else at["t"],)]]
+        return [whole_ref.at[(piece,) + index + (slice(None), half_lanes(tensor, half))] for tensor in tensors]
+
+    copies = []
+    for number, chain in enumerate(CHAINS):
+        copy = pltpu.make_async_copy(source(chain), views(chain, ())[0], own.at[number])
+        copy.start()
+        copies.append(copy)
+    flights = {}
+    for tick in range(5 + max(DELAYS)):
+        for number, chain in enumerate(CHAINS):
+            stage = tick - DELAYS[number]
+            if not 0 <= stage < 5:
+                continue
+            order = order_of(chain, GATHER_ORDERS)
+            targets = views(chain, order[:stage])
+            if stage == 0:
+                origins = [source(chain)]
+            else:
+                if stage == 1:
+                    copies[number].wait()
+                for flight in flights[number, stage - 1]:
+                    flight.wait_recv()
+                origins = targets
+            flights[number, stage] = []
+            for index, (origin, target) in enumerate(zip(origins, targets)):
+                flight = pltpu.make_async_remote_copy(
+                    src_ref=origin,
+                    dst_ref=target,
+                    send_sem=send.at[number, stage * 2 + index],
+                    recv_sem=recv.at[number, stage * 2 + index],
+                    device_id=partner(at, order[stage]),
+                    device_id_type=MESH,
+                )
+                flight.start()
+                flights[number, stage].append(flight)
+    for (number, stage), group in flights.items():
+        for flight in group:
+            if stage == 4:
+                flight.wait_recv()
+            flight.wait_send()
+
+
+def gather_fast(main, select, small):
+    anywhere = pl.BlockSpec(memory_space=pl.ANY)
+    inside = pl.BlockSpec(memory_space=pltpu.VMEM)
+    return pl.pallas_call(
+        gather_kernel,
+        in_specs=[inside] * 3,
+        out_specs=[anywhere] * 3,
+        out_shape=[
+            jax.ShapeDtypeStruct((3, 2, 2, 2, 2, 48, INNER), BF),
+            jax.ShapeDtypeStruct((2, 2, 2, 2, 2, 24, 2 * STATE), BF),
+            jax.ShapeDtypeStruct((2, 2, 2, 2, 2, 8, LANES), F32),
+        ],
+        scratch_shapes=[
+            pltpu.SemaphoreType.DMA((8, 10)),
+            pltpu.SemaphoreType.DMA((8, 10)),
+            pltpu.SemaphoreType.DMA((8,)),
+        ],
+        compiler_params=pltpu.CompilerParams(collective_id=0, has_side_effects=True),
+        name="gather_weights",
+    )(main, select, small)
+
+
+BUFFERS = 10
+
+
+def scatter_kernel(*refs):
+    grads, selects_ref, smalls_ref = refs[0:3], refs[3], refs[4]
+    main_out, select_out, small_out = refs[5:8]
+    send, recv, own = refs[8:11]
+    buffers = refs[11:]
+    at = places()
+    greet(at)
+
+    def sources(chain, core, target):
+        piece, half = chain
+        if chain in (SELECT, SMALL):
+            whole = selects_ref if chain == SELECT else smalls_ref
+            return [(whole.at[:, :, :, core], target)]
+        return [
+            (grads[piece].at[:, :, :, core, :, half_lanes(tensor, half)], target.at[:, :, :, tensor])
+            for tensor in range(2)
+        ]
+
+    copies = {}
+    for number, chain in enumerate(CHAINS):
+        copies[number] = []
+        for index, (origin, target) in enumerate(sources(chain, at["c"], buffers[number * BUFFERS])):
+            copy = pltpu.make_async_copy(origin, target, own.at[number, index])
+            copy.start()
+            copies[number].append(copy)
+    flights = {}
+
+    def start(number, stage):
+        chain = CHAINS[number]
+        order = order_of(chain, SCATTER_ORDERS)
+        arrived = buffers[number * BUFFERS + 1 + 2 * stage]
+        if stage == 0:
+            parts = sources(chain, 1 - at["c"], arrived)
+        else:
+            remaining = [axis for axis in AXES if axis not in order[1:stage]]
+            position = remaining.index(order[stage])
+            held = buffers[number * BUFFERS + 2 * stage]
+            parts = [(held.at[(slice(None),) * position + (1 - at[order[stage]],)], arrived)]
+        flights[number, stage] = []
+        for index, (origin, target) in enumerate(parts):
+            flight = pltpu.make_async_remote_copy(
+                src_ref=origin,
+                dst_ref=target,
+                send_sem=send.at[number, stage * 2 + index],
+                recv_sem=recv.at[number, stage * 2 + index],
+                device_id=partner(at, order[stage]),
+                device_id_type=MESH,
+            )
+            flight.start()
+            flights[number, stage].append(flight)
+
+    def finish(number, stage):
+        chain = CHAINS[number]
+        order = order_of(chain, SCATTER_ORDERS)
+        for flight in flights[number, stage]:
+            flight.wait_recv()
+        arrived = buffers[number * BUFFERS + 1 + 2 * stage]
+        if stage == 0:
+            for copy in copies[number]:
+                copy.wait()
+            mine, target = buffers[number * BUFFERS], buffers[number * BUFFERS + 2]
+            for index in range(8):
+                where = (index // 4, (index // 2) % 2, index % 2)
+                target[where] = (mine[where].astype(F32) + arrived[where].astype(F32)).astype(target.dtype)
+            return
+        remaining = [axis for axis in AXES if axis not in order[1:stage]]
+        position = remaining.index(order[stage])
+        held = buffers[number * BUFFERS + 2 * stage]
+        chosen = held[(slice(None),) * position + (at[order[stage]],)]
+        total = chosen.astype(F32) + arrived[...].astype(F32)
+        if stage < 4:
+            target = buffers[number * BUFFERS + 2 + 2 * stage]
+            target[...] = total.astype(target.dtype)
+        elif chain == SELECT:
+            select_out[...] = total
+        elif chain == SMALL:
+            small_out[...] = total
+        else:
+            main_out[chain[0], :, chain[1] * HALF : (chain[1] + 1) * HALF] = total
+
+    for tick in range(6 + max(DELAYS)):
+        for number in range(len(CHAINS)):
+            stage = tick - DELAYS[number]
+            if 0 < stage <= 5:
+                finish(number, stage - 1)
+            if 0 <= stage < 5:
+                start(number, stage)
+    for group in flights.values():
+        for flight in group:
+            flight.wait_send()
+
+
+def scatter_fast(first, second, third, select, small):
+    anywhere = pl.BlockSpec(memory_space=pl.ANY)
+    inside = pl.BlockSpec(memory_space=pltpu.VMEM)
+    scratch = [
+        pltpu.SemaphoreType.DMA((8, 10)),
+        pltpu.SemaphoreType.DMA((8, 10)),
+        pltpu.SemaphoreType.DMA((8, 2)),
+    ]
+    for chain in CHAINS:
+        block, kind = (48, HALF), BF
+        if chain == SELECT:
+            block = (24, 2 * STATE)
+        if chain == SMALL:
+            block, kind = (8, LANES), F32
+        for depth in (4, 4, 4, 3, 3, 2, 2, 1, 1, 0):
+            scratch.append(pltpu.VMEM((2,) * depth + block, kind))
+    return pl.pallas_call(
+        scatter_kernel,
+        in_specs=[anywhere] * 5,
+        out_specs=[inside] * 3,
+        out_shape=[
+            jax.ShapeDtypeStruct((3, 48, INNER // 2), F32),
+            jax.ShapeDtypeStruct((24, 2 * STATE), F32),
+            jax.ShapeDtypeStruct((8, LANES), F32),
+        ],
+        scratch_shapes=scratch,
+        compiler_params=pltpu.CompilerParams(
+            collective_id=1, has_side_effects=True, vmem_limit_bytes=VMEM_LIMIT
+        ),
+        name="scatter_gradients",
+    )(first, second, third, select, small)
+
+
 def gather_weights(shards):
     flat = jnp.concatenate([shard.reshape(-1) for shard in shards])
     everyone = lax.all_gather(flat, ("dp", "tensor"), axis=0, tiled=False)
@@ -564,19 +966,36 @@
     micro, rows = stream.shape[:2]
     chunks = rows // CHUNK
     assert rows * members == SLOT and bounds.shape[1] == 1
-    weights = (prescale, expansion, timestep, selection, kernels, biases, stencil, baseline, offset, decays, passthrough, rescale, readout)
-    got = gather_weights(weights)
-    prescale_full = got[0].reshape(WIDTH).astype(F32)
-    expand = join(got[1], 0, 2)
-    time_full = join(got[2], 0, 1)
-    select = got[3].reshape(WIDTH, 2 * STATE)
-    kernel_full = join(got[4], 1, 0).reshape(INNER, TAPS)
-    bias_full = join(got[5], 1, 0).reshape(INNER)
-    stencil_full = got[6].reshape(2 * STATE, TAPS)
-    baseline_full = got[7].reshape(2 * STATE)
-    offset_full, decays_full, pass_full = (item[0].reshape(HEADS).astype(F32) for item in got[8:11])
-    rescale_full = join(got[11], 1, 0).reshape(1, INNER).astype(F32)
-    readout_full = join(got[12], 1, 0)
+    fast = members == 2 and lax.axis_size("dp") == 16 and expansion.shape == (48, 2, 768)
+    small = (timestep, kernels, biases, rescale, prescale, stencil, baseline, offset, decays, passthrough)
+    if fast:
+        main = jnp.concatenate([jnp.swapaxes(expansion, 0, 1), readout.T[None]], axis=0)
+        packed = jnp.concatenate([item.reshape(-1).astype(F32) for item in small])
+        packed = jnp.pad(packed, (0, 8 * LANES - packed.shape[0])).reshape(8, LANES)
+        main, select, packed = gather_fast(main, selection, packed)
+        main = main.reshape(3, WIDTH, INNER)
+        gate_weight, inner_weight, readout_t = main[0], main[1], main[2]
+        select = select.reshape(WIDTH, 2 * STATE)
+        packed = packed.reshape(16, 2, 8 * LANES)
+        got = []
+        start = 0
+        for item in small:
+            got.append(packed[:, :, start : start + item.size].reshape((16, 2) + item.shape))
+            start += item.size
+    else:
+        got = gather_weights(small + (expansion, selection, readout))
+        expand = join(got[10], 0, 2)
+        gate_weight, inner_weight = expand[:, 0, :], expand[:, 1, :]
+        select = got[11].reshape(WIDTH, 2 * STATE)
+        readout_t = join(got[12], 1, 0).T
+    time_full = join(got[0], 0, 1).astype(BF)
+    kernel_full = join(got[1], 1, 0).reshape(INNER, TAPS)
+    bias_full = join(got[2], 1, 0).reshape(INNER)
+    rescale_full = join(got[3], 1, 0).reshape(1, INNER).astype(F32)
+    prescale_full = got[4].reshape(WIDTH).astype(F32)
+    stencil_full = got[5].reshape(2 * STATE, TAPS)
+    baseline_full = got[6].reshape(2 * STATE)
+    offset_full, decays_full, pass_full = (item[0].reshape(HEADS).astype(F32) for item in got[7:10])
 
     head = lax.broadcasted_iota(jnp.int32, (LANES, INNER), 0)
     channel = lax.broadcasted_iota(jnp.int32, (LANES, INNER), 1) // HEAD_DIM
@@ -600,8 +1019,7 @@
     edge = lax.ppermute(stream[:, rows - 8 :, :], "tensor", hops).reshape(micro * 8, WIDTH)
     lowered = low_norm(flat)
     lowered_edge = low_norm(edge)
-    signal_weight = jnp.concatenate([expand[:, 1, :], select], axis=1)
-    gate_weight = expand[:, 0, :]
+    signal_weight = jnp.concatenate([inner_weight, select], axis=1)
     time_weight = jnp.pad(time_full, ((0, 0), (0, LANES - HEADS)))
     signal = nn(lowered, signal_weight).astype(BF)
     signal_edge = nn(lowered_edge, signal_weight).astype(BF)
@@ -620,45 +1038,26 @@
     total_decay = decay[:, chunks - 1, 0:1, :]
     enter = chain(states[:, chunks - 1].astype(F32), total_decay, True)
 
-    reader = maps[:, STATE:]
-    high = reach.astype(BF)
-    reach_x = nn(high, gather.T) + nn((reach - high.astype(F32)).astype(BF), gather.T)
-    brought = jnp.einsum(
-        "min,mnk->mik", reader.reshape(micro, rows, STATE), enter, preferred_element_type=F32
-    ).reshape(micro * rows, INNER)
-    core = core + brought * reach_x
-    conv_f = convolved.astype(F32)
-    output = core + pass_wide * conv_f
-    gate_f = gate.astype(F32)
-    open_gate = jax.nn.sigmoid(gate_f)
-    silu = gate_f * open_gate
-    gated = output * silu
-    inverse = lax.rsqrt(jnp.mean(gated * gated, axis=1, keepdims=True) + EPS)
-    lifted = (gated * inverse * rescale_full).astype(BF)
-    live = cols[:, 6:7]
-    mixer = nn(lifted, readout_full)
-    result = (flat.astype(F32) + live * mixer).astype(BF)
     cot = cotangent.reshape(micro * rows, WIDTH)
-    back_mixer = jnp.where(live > 0, cot, jnp.zeros_like(cot))
-    readout_term = tn(lifted, back_mixer)
-    back_lifted = nt(back_mixer, readout_full)
-    rescale_term = jnp.sum(back_lifted * gated * inverse, axis=0)
-    weighted = back_lifted * rescale_full
-    dots = jnp.sum(weighted * gated, axis=1, keepdims=True)
-    back_gated = inverse * weighted - gated * (inverse * inverse * inverse) * (dots / INNER)
-    out = (back_gated * silu).astype(BF)
-    back_gate = (back_gated * output * open_gate * (1.0 + gate_f * (1.0 - open_gate))).astype(BF)
-    out_f = out.astype(F32)
-    pass_term = jnp.sum(jnp.sum(out_f * conv_f, axis=0).reshape(HEADS, HEAD_DIM), axis=1)
-    row_sums = jnp.sum((out_f * core).reshape(micro * rows, HEADS, HEAD_DIM), axis=2)
-    row_sums = jnp.pad(row_sums, ((0, 0), (0, LANES - HEADS)))
-    back_enter = jnp.einsum(
-        "min,mik->mnk",
-        reader.reshape(micro, rows, STATE),
-        (out_f * reach_x).astype(BF).reshape(micro, rows, INNER),
-        preferred_element_type=F32,
+    result, masked, lifted, out, back_gate, row_sums, back_enter, mix_acc = run_mixer(
+        core,
+        convolved,
+        gate,
+        maps,
+        reach,
+        enter,
+        cols,
+        flat,
+        cot,
+        readout_t,
+        taps,
+        jnp.broadcast_to(rescale_full, (8, INNER)),
+        spread,
+        gather,
+        micro,
     )
-    back = chain(back_enter, total_decay, False)
+    readout_term = tn(masked, lifted).astype(BF)
+    back = chain(back_enter.astype(F32), total_decay, False)
 
     grad_signal, back_raw, halo, acc, head_acc = run_backward(
         signal, tails, sraw, cols, segrow, taps, heads, spread, gather, out, row_sums, states, decay, enter, back, chunks
@@ -668,8 +1067,9 @@
     fixed = (grad_signal[:, rows - 8 :].astype(F32) + returned.astype(F32)).astype(BF)
     grad_signal = lax.dynamic_update_slice_in_dim(grad_signal, fixed, rows - 8, 1).reshape(micro * rows, CHANNELS)
 
-    gate_term = tn(lowered, back_gate)
-    signal_term = tn(lowered, grad_signal)
+    gate_term = tn(lowered, back_gate).astype(BF)
+    inner_term = tn(lowered, grad_signal[:, :INNER]).astype(BF)
+    select_term = tn(lowered, grad_signal[:, INNER:]).astype(BF)
     time_term = tn(lowered, back_raw)[:, :HEADS]
     back_lowered = nt(back_gate, gate_weight) + nt(grad_signal, signal_weight) + nt(back_raw, time_weight)
     values = flat.astype(F32)
@@ -682,39 +1082,70 @@
     sums = jnp.sum(acc.reshape(5, 8, CHANNELS), axis=1)
     tap_terms = jnp.stack([sums[4], sums[3], sums[2], sums[1]], axis=1)
     head_sums = jnp.sum(head_acc.reshape(2, 8, LANES), axis=1)[:, :HEADS]
-    grads = (
-        prescale_term[:, None],
-        jnp.stack([gate_term, signal_term[:, :INNER]], axis=1),
-        time_term,
-        signal_term[:, INNER:],
-        tap_terms[:INNER].reshape(HEADS, HEAD_DIM * TAPS),
-        sums[0, :INNER].reshape(HEADS, HEAD_DIM),
-        tap_terms[INNER:],
-        sums[0, INNER:][:, None],
-        rescale_term.reshape(HEADS, HEAD_DIM),
-        readout_term,
+    mix_sums = jnp.sum(mix_acc.reshape(2, 8, INNER), axis=1)
+    small_grads = (
+        (time_term, (0, 1)),
+        (tap_terms[:INNER].reshape(HEADS, HEAD_DIM * TAPS), (1, 0)),
+        (sums[0, :INNER].reshape(HEADS, HEAD_DIM), (1, 0)),
+        (mix_sums[0].reshape(HEADS, HEAD_DIM), (1, 0)),
+        (prescale_term, (0, 0)),
+        (tap_terms[INNER:], (0, 0)),
+        (sums[0, INNER:], (0, 0)),
     )
-    both = ((0, 0), (0, 2), (0, 1), (0, 0), (1, 0), (1, 0), (0, 0), (0, 0), (1, 0), (1, 0))
-    shapes = [item.shape for item in (prescale, expansion, timestep, selection, kernels, biases, stencil, baseline, rescale, readout)]
-    done = reduce_shards(grads, both, shapes)
-    scalars = lax.psum(jnp.stack([head_sums[0], head_sums[1], pass_term]), ("dp", "tensor"))
-    scalars = lax.dynamic_slice_in_dim(scalars, place * offset.shape[0], offset.shape[0], axis=1)
+    scalars = jnp.stack([head_sums[0], head_sums[1], jnp.sum(mix_sums[1].reshape(HEADS, HEAD_DIM), axis=1)])
+    shapes = [item.shape for item in small]
+    if fast:
+        scalars = jnp.swapaxes(scalars.reshape(3, 2, HEADS // 2), 0, 1).reshape(1, 2, -1)
+        packed = jnp.concatenate(
+            [cut(grad, *where).reshape(16, 2, -1) for grad, where in small_grads]
+            + [jnp.broadcast_to(scalars, (16,) + scalars.shape[1:])],
+            axis=2,
+        )
+        packed = jnp.pad(packed, ((0, 0), (0, 0), (0, 8 * LANES - packed.shape[2])))
+        square = lambda grad: grad.reshape(2, 2, 2, 2, 48, INNER)
+        main, select_grad, packed = scatter_fast(
+            square(readout_term),
+            square(gate_term),
+            square(inner_term),
+            select_term.reshape(2, 2, 2, 2, 2, 24, 2 * STATE),
+            packed.reshape(2, 2, 2, 2, 2, 8, LANES),
+        )
+        expansion_grad = jnp.stack([main[1], main[2]], axis=1)
+        readout_grad = main[0].T
+        packed = packed.reshape(-1)
+        done = []
+        start = 0
+        for item in small:
+            done.append(packed[start : start + item.size].reshape(item.shape))
+            start += item.size
+    else:
+        grads = [grad for grad, _ in small_grads] + [
+            jnp.stack([gate_term, inner_term], axis=1),
+            select_term,
+            readout_term.T,
+        ]
+        wheres = [where for _, where in small_grads] + [(0, 2), (0, 0), (1, 0)]
+        done = reduce_shards(grads, wheres, shapes[:7] + [expansion.shape, selection.shape, readout.shape])
+        expansion_grad, select_grad, readout_grad = done[7:]
+        scalars = lax.psum(scalars, ("dp", "tensor"))
+        scalars = lax.dynamic_slice_in_dim(scalars, place * offset.shape[0], offset.shape[0], axis=1)
+        done = done[:7] + [scalars[0], scalars[1], scalars[2]]
     return (
         result.reshape(stream.shape),
         grad_stream.reshape(stream.shape),
+        done[4],
+        expansion_grad,
         done[0],
+        select_grad,
         done[1],
         done[2],
-        done[3],
-        done[4],
         done[5],
         done[6],
         done[7],
-        scalars[0],
-        scalars[1],
-        scalars[2],
         done[8],
         done[9],
+        done[3],
+        readout_grad,
     )
 
 

time: 1020 us -> 504 us (0.49)
  waiting for transfers between devices: 278 us -> 34.4 us
  local copies, waits for them, and re-layouts: 314 us -> 71 us
  Pallas kernels: 125 us -> 269 us
  matrix products: 137 us -> 68.3 us
  blocking collectives: 44.6 us -> 0 us
  other arithmetic: 83.6 us -> 40.9 us
  between operations: 15.5 us -> 1.94 us
    unnamed x4 -> x0, waiting for transfers between devices: 261 us -> none
    pallas_call x0 -> x3, Pallas kernels: none -> 144 us  [the longest x1 52.6 us: scatter_fast(): pl.pallas_call(scatter_kernel, in_specs=[anywhere] * 5, out_specs=[inside...]
    reshape x27 -> x9, local copies, waits for them, and re-layouts: 86 us -> 5.58 us  [the longest x4 2.96 us: local(): cut(grad, *where).reshape(16, 2, -1)]
    unnamed x165 -> x151, local copies, waits for them, and re-layouts: 68.4 us -> 14.2 us
    dot_general x7 -> x4, matrix products: 62.2 us -> 16.7 us  [nn(): lax.dot_general(a, b, (((1,), (0,)), ((), ())), preferred_element_type=F32)]
    psum x1 -> x0, blocking collectives: 44.6 us -> none  [local(): lax.psum(jnp.stack([head_sums[0], head_sums[1], pass_term]), ('dp', 'tens...]
    reduce_sum x3 -> x2, other arithmetic: 28.7 us -> 0.16 us  [the longest x1 0.12 us: local(): jnp.sum(mix_sums[1].reshape(HEADS, HEAD_DIM), axis=1)]
    slice x31 -> x20, local copies, waits for them, and re-layouts: 38.5 us -> 14.8 us  [the longest x1 6.22 us: local(): gate_weight, inner_weight, readout_t = (main[0], main[1], main[2])]
  transfers between devices with their start and end apart: 6 -> 4, of which waited for: 3 -> 2; matrix products, arithmetic and copies ran while one was open for 15% -> 25% of each run, Pallas kernels for 0% -> 11%
where the time goes in v2:
time: 504 us; the launch traced here: 496 us
  Pallas kernels  269 us (53%)
  local copies, waits for them, and re-layouts  71 us (14%)
  matrix products  68.3 us (14%)
  other arithmetic  40.9 us (8%)
  waiting for transfers between devices  34.4 us (7%)
  starting transfers between devices  10.5 us (2%)
    pallas_call x1, Pallas kernels, run_backward(): pl.pallas_call(scan_backward, grid=(micro, chunks), in_specs=[flat(CHANNE...  87.9 us
    pallas_call x1, Pallas kernels, scatter_fast(): pl.pallas_call(scatter_kernel, in_specs=[anywhere] * 5, out_specs=[inside...  52.6 us
    pallas_call x1, Pallas kernels, gather_fast(): pl.pallas_call(gather_kernel, in_specs=[inside] * 3, out_specs=[anywhere]...  52.3 us
    pallas_call x1, Pallas kernels, run_mixer(): pl.pallas_call(mixer_kernel, grid=(micro, steps), in_specs=[flat(INNER),...  39.4 us
    pallas_call x1, Pallas kernels, run_forward(): pl.pallas_call(scan_forward, grid=(micro, chunks), in_specs=[flat(CHANNEL...  37 us
    ppermute x2, waiting for transfers between devices, chain(): held = lax.ppermute(value.astype(BF), 'tensor', hops)  34.4 us
    dot_general x5, matrix products, tn(): lax.dot_general(a, b, (((0,), (0,)), ((), ())), preferred_element_type=F32)  28.9 us
    dot_general x3, matrix products, nt(): lax.dot_general(a, b, (((1,), (1,)), ((), ())), preferred_element_type=F32)  22.7 us
  transfers between devices with their start and end apart: 4, of which 2 were waited for; matrix products, arithmetic and copies ran while one was open for 25% of the time, Pallas kernels for 11%

profile of v2, /device:TPU:0, one launch (start us, length us, event | category | flops | bytes accessed | tf_op | source)
XLA Modules:
  0.0 496.3 jit_solution(10974638412911956293)
XLA Ops:
  0.7 1.6 slice.163
  2.2 5.5 %collective-permute-start = (bf16[4,8,768]{2,1,0:T(8,128)(2,1)}, bf16[4,8,768]{2,1,0:T(8,128)(2,1)}, u32[]{:S(2)}, u32[]{:S(2)}) collective-permute-start(bf16[4,8,768]{2,1,0:T(8,128)(2,1)} %slice.163), channel_id=1, source_target_pairs={{0,1},{2,3},{4,5},{6,7},{8,9},{10,11},{12,13},{14,15},{16,17},{18,... | collective-permute-start | bytes 147464 | tf_op jit(solution)/shard_map/ppermute | solution.py:1019
  11.7 2.6 fusion
  19.5 3.4 concatenate.30
  23.5 1.6 pad_maximum_fusion.6.main_ref
  25.1 52.3 %gather_weights.1 = (bf16[3,2,2,2,2,48,1536]{6,5,4,3,2,1,0:T(8,128)(2,1)}, bf16[2,2,2,2,2,24,256]{6,5,4,3,2,1,0:T(8,128)(2,1)}, f32[2,2,2,2,2,8,128]{6,5,4,3,2,1,0:T(8,128)}) custom-call(bf16[3,48,768]{2,1,0:T(8,128)(2,1)} %pad_maximum_fusion.6.main_ref, bf16[24,256]{1,0:T(8,128)(2,1)} %select_ref.1, f32[8,128]{1,0:T(8,128)} %bitcast_convert_fusion.small_ref), custom_call_target="tpu_custom_call" | custom-call | tf_op jit(solution)/shard_map/gather_weights/pallas_call | solution.py:695
  91.8 2.5 fusion.4
  94.2 6.2 %fusion.67 = (bf16[1,2,2,2,2,48,1536]{6,5,4,3,2,1,0:T(8,128)(2,1)}, bf16[1,2,2,2,2,48,1536]{6,5,4,3,2,1,0:T(8,128)(2,1)}, bf16[1,2,2,2,2,48,1536]{6,5,4,3,2,1,0:T(8,128)(2,1)}) fusion(bf16[3,2,2,2,2,48,1536]{6,5,4,3,2,1,0:T(8,128)(2,1)} %get-tuple-element.41), kind=kLoop, calls=%fused_computation.168 | loop fusion | bytes 14155776 | tf_op jit(solution)/shard_map/slice | solution.py:977
  102.5 2.0 reshape_reshape.16
  104.5 2.0 copy.89
  109.5 1.2 convert_element_type.343
  111.6 1.1 convert_element_type.345
  115.7 3.3 fusion.2
  119.8 2.0 fusion.28.sraw_ref
  122.1 6.3 %convolution_convert_fusion.1.x_ref = bf16[2048,1792]{1,0:T(8,128)(2,1)S(1)} fusion(bf16[2048,768]{1,0:T(8,128)(2,1)S(1)} %copy-done.2, bf16[768,256]{1,0:T(8,128)(2,1)S(1)} %bitcast.254, bf16[768,1536]{1,0:T(8,128)(2,1)S(1)} %bitcast.196), kind=kOutput, calls=%fused_computation.7 | convolution fusion | flops 5646319616 | bytes 13238272 | tf_op jit(solution)/shard_map/dot_general | solution.py:28
  129.5 1.5 fusion.21.spread_ref
  131.3 3.3 select_select_fusion.cols_ref
  136.7 1.7 fusion.17
  139.8 37.0 %scan_forward.1 = (f32[2048,1536]{1,0:T(8,128)}, bf16[2048,1536]{1,0:T(8,128)(2,1)}, bf16[2048,256]{1,0:T(8,128)(2,1)}, f32[2048,128]{1,0:T(8,128)}, bf16[4,4,12...) custom-call(bf16[2048,1792]{1,0:T(8,128)(2,1)} %copy-done.5, bf16[16,8,1792]{2,1,0:T(8,128)(2,1)} %bitcast.190, ...), custom_call_target="tpu_custom_call" | custom-call | tf_op jit(solution)/shard_map/scan_forward/pallas_call | solution.py:357
  176.9 1.5 slice_bitcast_fusion
  178.4 2.5 collective-permute-start.1
  180.9 2.2 fusion.23.gather_ref
  183.0 6.8 %convolution_convert_fusion.gate_ref = bf16[2048,1536]{1,0:T(8,128)(2,1)} fusion(bf16[2048,768]{1,0:T(8,128)(2,1)S(1)} %bitcast.192, bf16[768,1536]{1,0:T(8,128)(2,1)S(1)} %bitcast.198), kind=kOutput, calls=%fused_computation.6 | convolution fusion | flops 4834983936 | bytes 11796480 | tf_op jit(solution)/shard_map/dot_general | solution.py:28
  189.9 25.0 %collective-permute-done.1.enter_ref = bf16[4,128,1536]{2,1,0:T(8,128)(2,1)S(1)} collective-permute-done((bf16[4,128,1536]{2,1,0:T(8,128)(2,1)S(1)}, bf16[4,128,1536]{2,1,0:T(8,128)(2,1)S(1)}, u32[]{:S(2)}, u32[]{:S(2)}) %collective-permute-start.1) | collective-permute-done | bytes 1572896 | tf_op jit(solution)/shard_map/ppermute | solution.py:913
  216.1 39.4 %gated_mixer.1 = (bf16[2048,768]{1,0:T(8,128)(2,1)}, bf16[2048,768]{1,0:T(8,128)(2,1)}, bf16[2048,1536]{1,0:T(8,128)(2,1)}, bf16[2048,1536]{1,0:T(8,128)(2,1)}, ...) custom-call(f32[2048,1536]{1,0:T(8,128)} %get-tuple-element.43.core_ref, ...), custom_call_target="tpu_custom_call" | custom-call | tf_op jit(solution)/shard_map/gated_mixer/pallas_call | solution.py:547
  255.5 1.3 collective-permute-start.2
  256.9 9.7 %convolution_convert_fusion.2 = bf16[768,1536]{1,0:T(8,128)(2,1)} fusion(bf16[2048,768]{1,0:T(8,128)(2,1)S(1)} %copy-done.3, bf16[2048,1536]{1,0:T(8,128)(2,1)} %get-tuple-element.49), kind=kOutput, calls=%fused_computation.24 | convolution fusion | flops 4833017856 | bytes 11796480 | tf_op jit(solution)/shard_map/dot_general | solution.py:36
  266.6 7.0 %fusion.72 = f32[2048,768]{1,0:T(8,128)} fusion(bf16[2048,1536]{1,0:T(8,128)(2,1)S(1)} %copy-done.58, bf16[768,1536]{1,0:T(8,128)(2,1)S(1)} %bitcast.199), kind=kOutput, calls=%fused_computation.173 | convolution fusion | flops 4831838208 | bytes 14942208 | tf_op jit(solution)/shard_map/dot_general | solution.py:32
  275.1 9.3 %convolution_convert_fusion.3 = bf16[768,1536]{1,0:T(8,128)(2,1)} fusion(bf16[2048,768]{1,0:T(8,128)(2,1)} %get-tuple-element.57, bf16[2048,1536]{1,0:T(8,128)(2,1)} %get-tuple-element.58), kind=kOutput, calls=%fused_computation.25 | convolution fusion | flops 4833017856 | bytes 11796480 | tf_op jit(solution)/shard_map/dot_general | solution.py:36
  284.4 9.3 %collective-permute-done.2.back_ref = bf16[4,128,1536]{2,1,0:T(8,128)(2,1)} collective-permute-done((bf16[4,128,1536]{2,1,0:T(8,128)(2,1)}, bf16[4,128,1536]{2,1,0:T(8,128)(2,1)}, u32[]{:S(2)}, u32[]{:S(2)}) %collective-permute-start.2) | collective-permute-done | bytes 1572896 | tf_op jit(solution)/shard_map/ppermute | solution.py:913
  293.7 87.9 %scan_backward.1 = (bf16[2048,1792]{1,0:T(8,128)(2,1)}, bf16[2048,128]{1,0:T(8,128)(2,1)}, bf16[4,8,1792]{2,1,0:T(8,128)(2,1)}, f32[40,1792]{1,0:T(8,128)}, f32[16,128]{1,0:T(8,128)}) custom-call(bf16[2048,1792]{1,0:T(8,128)(2,1)} %copy-done.5, bf16[16,8,1792]{2,1,0:T(8,128)(2,1)} %bitcast.191, f32[2048,128]{1,0:T(8,128)} %fusion.28.sraw_ref, ...), custom_call_target="tpu_custom_call" | custom-call | tf_op jit(solution)/shard_map/scan_backward/pallas_call | solution.py:397
  384.1 1.3 collective-permute-start.3
  385.4 1.6 fusion.24
  388.0 1.3 copy.97
  389.2 2.0 reshape_reshape.19
  393.1 1.3 copy.96
  394.4 1.5 reshape.1199
  397.9 1.6 fusion.32
  399.5 9.3 %fusion.19 = f32[2048,768]{1,0:T(8,128)S(1)} fusion(bf16[2048,1792]{1,0:T(8,128)(2,1)} %bitcast.248, bf16[768,256]{1,0:T(8,128)(2,1)} %bitcast.253, bf16[768,1536]{1,0:T(8,128)(2,1)} %bitcast.195), kind=kOutput, calls=%fused_computation.33 | convolution fusion | flops 5642649600 | bytes 16384000 | tf_op jit(solution)/shard_map/dot_general | solution.py:32
  408.9 6.5 %fusion.14 = bf16[768,1536]{1,0:T(8,128)(2,1)} fusion(bf16[2048,768]{1,0:T(8,128)(2,1)S(1)} %copy-done.3, bf16[2048,1792]{1,0:T(8,128)(2,1)S(1)} %bitcast.249), kind=kOutput, calls=%fused_computation.23 | convolution fusion | flops 4833017856 | bytes 11796480 | tf_op jit(solution)/shard_map/dot_general | solution.py:36
  415.4 1.8 convolution_convert_fusion.5
  417.5 6.3 %fusion.11 = (f32[768]{0:T(1024)S(1)}, f32[2048]{0:T(1024)S(1)}, f32[2048,768]{1,0:T(8,128)}) fusion(f32[2048]{0:T(1024)S(1)} %bitcast.214, bf16[4,512,768]{2,1,0:T(8,128)(2,1)S(1)} %copy-done.1, f32[768]{0:T(1024)S(1)} %mul.116, bf16[2048,128]{1,0:T(8,128)(2,1)S(1)} %copy-done.12, bf16[768,24]{0,1:T(8,128)(2,1)S(1)} %convert_element_type.345, ...), kind=kOutput, calls=%fused_computation.19 | convolution fusion | flops 416806144 | bytes 22603776 | tf_op jit(solution)/shard_map/dot_general | solution.py:32
  424.9 52.6 %scatter_gradients.1 = (f32[3,48,768]{2,1,0:T(8,128)}, f32[24,256]{1,0:T(8,128)}, f32[8,128]{1,0:T(8,128)}) custom-call(bf16[2,2,2,2,48,1536]{5,4,3,2,1,0:T(8,128)(2,1)} %bitcast.201, bf16[2,2,2,2,48,1536]{5,4,3,2,1,0:T(8,128)(2,1)} %bitcast.200, bf16[2,2,2,2,48,1536]{5,4,3,2,1,0:T(8,128)(2,1)} %bitcast.202, bf16[2,2,2,2,2,24,256]{6,5,4,3,2,1,0:T(8,128)(2,1)} %bitcast.211, ...), custom_call_target="tpu_custom_call" | custom-call | tf_op jit(solution)/shard_map/scatter_gradients/pallas_call | solution.py:825
  479.0 1.4 fusion.71
  480.4 1.3 slice.194
  481.6 1.3 slice.203
  482.9 1.7 slice_bitcast_fusion.1
  489.6 5.9 %fusion.8 = bf16[2048,768]{1,0:T(8,128)(2,1)} fusion(f32[2048,768]{1,0:T(8,128)} %get-tuple-element.147, f32[2048]{0:T(1024)S(1)} %broadcast_multiply_fusion, f32[2048]{0:T(1024)S(1)} %copy-done.24, f32[768]{0:T(1024)S(1)} %mul.116, f32[2048]{0:T(1024)S(1)} %bitcast.215, bf16[4,512,768]{2,1,0:T(8,128)(2,1)} %param.31, bf16[4,512,768]{2,1,0:T(8,128)(2,1)S(1)} %copy-done.1), kind=kLoop, calls=%fused_computation.16 | loop fusion | flops 14155776 | bytes 15756288 | tf_op jit(solution)/shard_map/convert_element_type | solution.py:1080
  (285 shorter events, 56.9 us)
Async XLA Ops:
  0.6 91.1 %copy-start = (bf16[4,512,768]{2,1,0:T(8,128)(2,1)S(1)}, bf16[4,512,768]{2,1,0:T(8,128)(2,1)}, u32[]{:S(2)}) copy-start(bf16[4,512,768]{2,1,0:T(8,128)(2,1)} %param.16) | copy-start | bytes 9437188
  2.2 133.5 %collective-permute-start = (bf16[4,8,768]{2,1,0:T(8,128)(2,1)}, bf16[4,8,768]{2,1,0:T(8,128)(2,1)}, u32[]{:S(2)}, u32[]{:S(2)}) collective-permute-start(bf16[4,8,768]{2,1,0:T(8,128)(2,1)} %slice.163), channel_id=1, source_target_pairs={{0,1},{2,3},{4,5},{6,7},{8,9},{10,11},{12,13},{14,15},{16,17},{18,... | collective-permute-start | bytes 147464 | tf_op jit(solution)/shard_map/ppermute | solution.py:1019
  85.0 15.5 %copy-start.42 = (s32[4]{0:T(128)}, s32[4]{0:T(128)S(1)}, u32[]{:S(2)}) copy-start(s32[4]{0:T(128)S(1)} %get-tuple-element.145) | copy-start | bytes 52
  85.0 15.5 %copy-start.43 = (s32[4]{0:T(128)}, s32[4]{0:T(128)S(1)}, u32[]{:S(2)}) copy-start(s32[4]{0:T(128)S(1)} %get-tuple-element.146) | copy-start | bytes 52
  111.6 8.1 %copy-start.17 = (s32[1,4,4,128]{3,1,2,0:T(4,128)S(1)}, s32[1,4,4,128]{3,1,2,0:T(4,128)}, u32[]{:S(2)}) copy-start(s32[1,4,4,128]{3,1,2,0:T(4,128)} %copy.118) | copy-start | bytes 24580
  111.6 8.1 %copy-start.18 = (s32[1,4,4,128]{3,1,2,0:T(4,128)S(1)}, s32[1,4,4,128]{3,1,2,0:T(4,128)}, u32[]{:S(2)}) copy-start(s32[1,4,4,128]{3,1,2,0:T(4,128)} %copy.119) | copy-start | bytes 24580
  111.6 8.1 %copy-start.25 = (s32[1,4,4,128]{3,1,2,0:T(4,128)S(1)}, s32[1,4,4,128]{3,1,2,0:T(4,128)}, u32[]{:S(2)}) copy-start(s32[1,4,4,128]{3,1,2,0:T(4,128)} %copy.120) | copy-start | bytes 24580
  121.8 7.6 %copy-start.36 = (s32[4,128]{1,0:T(4,128)S(1)}, s32[4,128]{1,0:T(4,128)}, u32[]{:S(2)}) copy-start(s32[4,128]{1,0:T(4,128)} %add_add_fusion.1) | copy-start | bytes 6148
  121.8 7.6 %copy-start.57 = (pred[4,128]{1,0:T(4,128)(4,1)S(1)}, pred[4,128]{1,0:T(4,128)(4,1)}, u32[]{:S(2)}) copy-start(pred[4,128]{1,0:T(4,128)(4,1)} %broadcast_compare_fusion) | copy-start | bytes 1540
  121.8 7.7 %copy-start.19 = (s32[1536]{0:T(1024)S(1)}, s32[1536]{0:T(1024)}, u32[]{:S(2)}) copy-start(s32[1536]{0:T(1024)} %broadcast_add_fusion) | copy-start | bytes 18436
  121.8 7.7 %copy-start.20 = (s32[1536]{0:T(1024)S(1)}, s32[1536]{0:T(1024)}, u32[]{:S(2)}) copy-start(s32[1536]{0:T(1024)} %iota_shift-right-logical_fusion) | copy-start | bytes 18436
  121.8 7.7 %copy-start.29 = (pred[1536]{0:T(1024)(128)(4,1)S(1)}, pred[1536]{0:T(1024)(128)(4,1)}, u32[]{:S(2)}) copy-start(pred[1536]{0:T(1024)(128)(4,1)} %fusion.50) | copy-start | bytes 4612
  121.8 7.7 %copy-start.53 = (pred[128]{0:T(512)(128)(4,1)S(1)}, pred[128]{0:T(512)(128)(4,1)}, u32[]{:S(2)}) copy-start(pred[128]{0:T(512)(128)(4,1)} %get-tuple-element.170) | copy-start | bytes 388
  121.8 7.7 %copy-start.54 = (pred[128]{0:T(512)(128)(4,1)S(1)}, pred[128]{0:T(512)(128)(4,1)}, u32[]{:S(2)}) copy-start(pred[128]{0:T(512)(128)(4,1)} %get-tuple-element.171) | copy-start | bytes 388
  121.9 7.7 %copy-start.55 = (s32[128]{0:T(128)S(1)}, s32[128]{0:T(128)}, u32[]{:S(2)}) copy-start(s32[128]{0:T(128)} %get-tuple-element.172) | copy-start | bytes 1540
  121.9 7.7 %copy-start.56 = (s32[128]{0:T(128)S(1)}, s32[128]{0:T(128)}, u32[]{:S(2)}) copy-start(s32[128]{0:T(128)} %get-tuple-element.173) | copy-start | bytes 1540
  121.9 9.1 %copy-start.41 = (s32[512]{0:T(512)S(1)}, s32[512]{0:T(512)}, u32[]{:S(2)}) copy-start(s32[512]{0:T(512)} %get-tuple-element.155) | copy-start | bytes 6148
  121.9 9.1 %copy-start.40 = (s32[512]{0:T(512)S(1)}, s32[512]{0:T(512)}, u32[]{:S(2)}) copy-start(s32[512]{0:T(512)} %get-tuple-element.154) | copy-start | bytes 6148
  121.9 9.2 %copy-start.39 = (s32[512]{0:T(512)S(1)}, s32[512]{0:T(512)}, u32[]{:S(2)}) copy-start(s32[512]{0:T(512)} %get-tuple-element.151) | copy-start | bytes 6148
  121.9 9.2 %copy-start.38 = (s32[512]{0:T(512)S(1)}, s32[512]{0:T(512)}, u32[]{:S(2)}) copy-start(s32[512]{0:T(512)} %get-tuple-element.150) | copy-start | bytes 6148
  121.9 9.2 %copy-start.37 = (s32[512]{0:T(512)S(1)}, s32[512]{0:T(512)}, u32[]{:S(2)}) copy-start(s32[512]{0:T(512)} %get-tuple-element.149) | copy-start | bytes 6148
  121.9 9.2 %copy-start.31 = (pred[1,4,4,128]{3,1,2,0:T(4,128)(4,1)S(1)}, pred[1,4,4,128]{3,1,2,0:T(4,128)(4,1)}, u32[]{:S(2)}) copy-start(pred[1,4,4,128]{3,1,2,0:T(4,128)(4,1)} %copy.121) | copy-start | bytes 6148
  121.9 9.2 %copy-start.32 = (pred[1,4,4,128]{3,1,2,0:T(4,128)(4,1)S(1)}, pred[1,4,4,128]{3,1,2,0:T(4,128)(4,1)}, u32[]{:S(2)}) copy-start(pred[1,4,4,128]{3,1,2,0:T(4,128)(4,1)} %copy.122) | copy-start | bytes 6148
  121.9 9.2 %copy-start.33 = (pred[1,4,4,128]{3,1,2,0:T(4,128)(4,1)S(1)}, pred[1,4,4,128]{3,1,2,0:T(4,128)(4,1)}, u32[]{:S(2)}) copy-start(pred[1,4,4,128]{3,1,2,0:T(4,128)(4,1)} %copy.123) | copy-start | bytes 6148
  122.0 9.2 %copy-start.34 = (pred[1,4,4,128]{3,1,2,0:T(4,128)(4,1)S(1)}, pred[1,4,4,128]{3,1,2,0:T(4,128)(4,1)}, u32[]{:S(2)}) copy-start(pred[1,4,4,128]{3,1,2,0:T(4,128)(4,1)} %copy.124) | copy-start | bytes 6148
  122.0 9.2 %copy-start.35 = (pred[1,4,4,128]{3,1,2,0:T(4,128)(4,1)S(1)}, pred[1,4,4,128]{3,1,2,0:T(4,128)(4,1)}, u32[]{:S(2)}) copy-start(pred[1,4,4,128]{3,1,2,0:T(4,128)(4,1)} %copy.125) | copy-start | bytes 6148
  122.0 9.2 %copy-start.45 = (pred[128]{0:T(512)(128)(4,1)S(1)}, pred[128]{0:T(512)(128)(4,1)}, u32[]{:S(2)}) copy-start(pred[128]{0:T(512)(128)(4,1)} %get-tuple-element.162) | copy-start | bytes 388
  122.0 9.2 %copy-start.46 = (pred[128]{0:T(512)(128)(4,1)S(1)}, pred[128]{0:T(512)(128)(4,1)}, u32[]{:S(2)}) copy-start(pred[128]{0:T(512)(128)(4,1)} %get-tuple-element.163) | copy-start | bytes 388
  122.0 9.2 %copy-start.47 = (pred[128]{0:T(512)(128)(4,1)S(1)}, pred[128]{0:T(512)(128)(4,1)}, u32[]{:S(2)}) copy-start(pred[128]{0:T(512)(128)(4,1)} %get-tuple-element.164) | copy-start | bytes 388
  122.0 9.2 %copy-start.48 = (pred[128]{0:T(512)(128)(4,1)S(1)}, pred[128]{0:T(512)(128)(4,1)}, u32[]{:S(2)}) copy-start(pred[128]{0:T(512)(128)(4,1)} %get-tuple-element.165) | copy-start | bytes 388
  122.0 9.2 %copy-start.49 = (pred[128]{0:T(512)(128)(4,1)S(1)}, pred[128]{0:T(512)(128)(4,1)}, u32[]{:S(2)}) copy-start(pred[128]{0:T(512)(128)(4,1)} %get-tuple-element.166) | copy-start | bytes 388
  122.0 9.2 %copy-start.50 = (pred[128]{0:T(512)(128)(4,1)S(1)}, pred[128]{0:T(512)(128)(4,1)}, u32[]{:S(2)}) copy-start(pred[128]{0:T(512)(128)(4,1)} %get-tuple-element.167) | copy-start | bytes 388
  122.0 9.2 %copy-start.51 = (pred[128]{0:T(512)(128)(4,1)S(1)}, pred[128]{0:T(512)(128)(4,1)}, u32[]{:S(2)}) copy-start(pred[128]{0:T(512)(128)(4,1)} %get-tuple-element.168) | copy-start | bytes 388
  122.1 9.2 %copy-start.52 = (pred[128]{0:T(512)(128)(4,1)S(1)}, pred[128]{0:T(512)(128)(4,1)}, u32[]{:S(2)}) copy-start(pred[128]{0:T(512)(128)(4,1)} %get-tuple-element.169) | copy-start | bytes 388
  122.1 13.2 %copy-start.21 = (f32[16,2,48]{2,1,0:T(2,128)S(1)}, f32[16,2,48]{2,1,0:T(2,128)}, u32[]{:S(2)}) copy-start(f32[16,2,48]{2,1,0:T(2,128)} %get-tuple-element.125) | copy-start | bytes 18436
  122.1 14.6 %copy-start.9 = (bf16[1,2,2,2,2,48,1536]{6,5,4,3,2,1,0:T(8,128)(2,1)S(1)}, bf16[1,2,2,2,2,48,1536]{6,5,4,3,2,1,0:T(8,128)(2,1)}, u32[]{:S(2)}) copy-start(bf16[1,2,2,2,2,48,1536]{6,5,4,3,2,1,0:T(8,128)(2,1)} %get-tuple-element.119) | copy-start | bytes 7077892
  128.4 6.8 %copy-start.5 = (bf16[2048,1792]{1,0:T(8,128)(2,1)}, bf16[2048,1792]{1,0:T(8,128)(2,1)S(1)}, u32[]{:S(2)}) copy-start(bf16[2048,1792]{1,0:T(8,128)(2,1)S(1)} %convolution_convert_fusion.1.x_ref) | copy-start | bytes 22020100
  139.8 43.2 %copy-start.7 = (bf16[4,512,768]{2,1,0:T(8,128)(2,1)S(1)}, bf16[4,512,768]{2,1,0:T(8,128)(2,1)}, u32[]{:S(2)}) copy-start(bf16[4,512,768]{2,1,0:T(8,128)(2,1)} %fusion.2) | copy-start | bytes 9437188
  139.8 43.2 %copy-start.10 = (bf16[1,2,2,2,2,48,1536]{6,5,4,3,2,1,0:T(8,128)(2,1)S(1)}, bf16[1,2,2,2,2,48,1536]{6,5,4,3,2,1,0:T(8,128)(2,1)}, u32[]{:S(2)}) copy-start(bf16[1,2,2,2,2,48,1536]{6,5,4,3,2,1,0:T(8,128)(2,1)} %get-tuple-element.118) | copy-start | bytes 7077892
  178.4 36.5 %collective-permute-start.1 = (bf16[4,128,1536]{2,1,0:T(8,128)(2,1)S(1)}, bf16[4,128,1536]{2,1,0:T(8,128)(2,1)S(1)}, u32[]{:S(2)}, u32[]{:S(2)}) collective-permute-start(bf16[4,128,1536]{2,1,0:T(8,128)(2,1)S(1)} %slice_bitcast_fusion), channel_id=1, source_target_pairs={{0,1},{2,3},{4,5},{6,7},{8,9},{10,11},{12,13},{14,15},{16,17},{18,... | collective-permute-start | bytes 4718600 | tf_op jit(solution)/shard_map/ppermute | solution.py:913
  216.1 40.7 %copy-start.3 = (bf16[2048,768]{1,0:T(8,128)(2,1)S(1)}, bf16[2048,768]{1,0:T(8,128)(2,1)}, u32[]{:S(2)}) copy-start(bf16[2048,768]{1,0:T(8,128)(2,1)} %fusion.4) | copy-start | bytes 9437188
  255.5 38.1 %collective-permute-start.2 = (bf16[4,128,1536]{2,1,0:T(8,128)(2,1)}, bf16[4,128,1536]{2,1,0:T(8,128)(2,1)}, u32[]{:S(2)}, u32[]{:S(2)}) collective-permute-start(bf16[4,128,1536]{2,1,0:T(8,128)(2,1)} %get-tuple-element.53), channel_id=1, source_target_pairs={{1,0},{3,2},{5,4},{7,6},{9,8},{11,10},{13,12},{15,14},{17,16},{19,... | collective-permute-start | bytes 4718600 | tf_op jit(solution)/shard_map/ppermute | solution.py:913
  256.8 9.8 %copy-start.11 = (bf16[1,2,2,2,2,48,1536]{6,5,4,3,2,1,0:T(8,128)(2,1)S(1)}, bf16[1,2,2,2,2,48,1536]{6,5,4,3,2,1,0:T(8,128)(2,1)}, u32[]{:S(2)}) copy-start(bf16[1,2,2,2,2,48,1536]{6,5,4,3,2,1,0:T(8,128)(2,1)} %get-tuple-element.118) | copy-start | bytes 7077892
  256.8 9.7 %copy-start.58 = (bf16[2048,1536]{1,0:T(8,128)(2,1)S(1)}, bf16[2048,1536]{1,0:T(8,128)(2,1)}, u32[]{:S(2)}) copy-start(bf16[2048,1536]{1,0:T(8,128)(2,1)} %get-tuple-element.49) | copy-start | bytes 18874372
  266.6 7.0 %copy-start.16 = (f32[16,1536]{1,0:T(8,128)S(1)}, f32[16,1536]{1,0:T(8,128)}, u32[]{:S(2)}) copy-start(f32[16,1536]{1,0:T(8,128)} %get-tuple-element.60) | copy-start | bytes 294916
  384.1 13.8 %collective-permute-start.3 = (bf16[4,8,1792]{2,1,0:T(8,128)(2,1)}, bf16[4,8,1792]{2,1,0:T(8,128)(2,1)}, u32[]{:S(2)}, u32[]{:S(2)}) collective-permute-start(bf16[4,8,1792]{2,1,0:T(8,128)(2,1)} %get-tuple-element.55), channel_id=1, source_target_pairs={{1,0},{3,2},{5,4},{7,6},{9,8},{11,10},{13,12},{15,14},{17,16},{19,... | collective-permute-start | bytes 344072 | tf_op jit(solution)/shard_map/ppermute | solution.py:1065
  399.5 9.3 %copy-start.44 = (bf16[4,512,1792]{2,1,0:T(8,128)(2,1)S(1)}, bf16[4,512,1792]{2,1,0:T(8,128)(2,1)}, u32[]{:S(2)}) copy-start(bf16[4,512,1792]{2,1,0:T(8,128)(2,1)} %fusion.32) | copy-start | bytes 22020100
  424.0 65.6 %copy-start.24 = (f32[2048]{0:T(1024)S(1)}, f32[2048]{0:T(1024)}, u32[]{:S(2)}) copy-start(f32[2048]{0:T(1024)} %multiply_multiply_fusion) | copy-start | bytes 24580
  (16 other events, 82.6 us)
